TPU v7x, 16 devices: a whole 2x2x2 slice. The times are simulated.
16 devices in a mesh: rep: 1, r: 4 (over y, z), s: 4 (over x, core).
Axes of the slice: x: 2, y: 2, z: 2, core: 2. Of those that a mesh axis runs over, the one named last changes fastest.
Arguments:
- x: bfloat16 [16, 4096, 1024], P(('rep', 'r', 's'))
- dy: bfloat16 [16, 4096, 1024], P(('rep', 'r', 's'))
- w_gate: bfloat16 [2, 1024, 3200], P(None, 's')
- w_up: bfloat16 [2, 1024, 3200], P(None, 's')
- w_down: bfloat16 [2, 3200, 1024], P(None, 's')
Outputs:
- output 1: bfloat16 [16, 4096, 1024], P(('rep', 'r', 's'))
- output 2: bfloat16 [2, 1024, 3200], P('rep', 's')
- output 3: bfloat16 [2, 1024, 3200], P('rep', 's')
- output 4: bfloat16 [2, 3200, 1024], P('rep', 's')
All inputs are finite; a program needn't handle non-finite values.
Results may differ from a plain program's by a relative error of at most 0.018.
Values are sent between devices in bfloat16 or wider.
A program may use at most 2 GiB of HBM per device.

v0:
```python
import jax
import jax.numpy as jnp
from jax import lax
from jax.sharding import PartitionSpec as P

NAMES = ("w_gate", "w_up", "w_down")


def matmul(a, w):
    return jnp.dot(a, w, preferred_element_type=jnp.float32).astype(jnp.bfloat16)


def normed(h):
    wide = h.astype(jnp.float32)
    scale = lax.rsqrt(jnp.mean(wide**2, -1, keepdims=True) + 1e-6)
    return (wide * scale).astype(jnp.bfloat16)


def layer(h, w):
    a = normed(h)
    gate = jnp.dot(a, w["w_gate"], preferred_element_type=jnp.float32)
    up = jnp.dot(a, w["w_up"], preferred_element_type=jnp.float32)
    return h + matmul((jax.nn.silu(gate) * up).astype(jnp.bfloat16), w["w_down"])


def solution(mesh):
    def fetched(weights, number):
        return {name: lax.all_gather(w[number], "s", axis=0, tiled=True) for name, w in zip(NAMES, weights, strict=True)}

    def summed(term):
        return lax.psum(lax.psum_scatter(term, "s", scatter_dimension=0, tiled=True), "r")

    def step(x, dy, *weights):
        layers = weights[0].shape[0]
        h, inputs = x[0], []
        for number in range(layers):
            inputs.append(h)
            h = layer(h, fetched(weights, number))
        by_h, mine = dy[0], [None] * layers
        for number in reversed(range(layers)):
            _, back = jax.vjp(lambda w, h: layer(h, w), fetched(weights, number), inputs[number])
            by_w, by_h = back(by_h)
            mine[number] = [summed(by_w[name]) for name in NAMES]
        return (by_h[None], *(jnp.stack([mine[number][i] for number in range(layers)]) for i in range(3)))

    states, cut = P(("rep", "r", "s"), None, None), P(None, "s", None)
    return jax.shard_map(
        step,
        mesh=mesh,
        in_specs=(states, states) + (cut,) * 3,
        out_specs=(states,) + (P("rep", "s", None),) * 3,
        check_vma=False,
    )
```

profile of v0, /device:TPU:0, one launch (start us, length us, event | category | flops | bytes accessed | tf_op | source)
XLA Modules:
  0.0 1084.1 jit_solution(11597077321648331380)
XLA Ops:
  7.2 4.0 fusion.65
  19.2 11.9 %copy.10 = bf16[1,4096,1024]{1,2,0:T(8,128)(2,1)} copy(bf16[1,4096,1024]{2,1,0:T(8,128)(2,1)} %param.5) | data formatting | bytes 16777216 | tf_op args[0]
  31.1 5.1 fusion.15
  36.8 11.6 %copy.9 = bf16[1,4096,1024]{1,2,0:T(8,128)(2,1)} copy(bf16[1,4096,1024]{2,1,0:T(8,128)(2,1)} %param.6) | data formatting | bytes 16777216 | tf_op args[1]
  48.3 11.9 %all-gather.13.cloned.1.call-done = bf16[1,1024,3200]{2,1,0:T(8,128)(2,1)} async-done(((bf16[1,256,3200]{2,1,0:T(8,128)(2,1)}), bf16[1,1024,3200]{2,1,0:T(8,128)(2,1)}) %all-gather.13.cloned.1.call-update) | async-done | bytes 6553616 | tf_op jit(solution)/shard_map/all_gather | solution.py:28
  60.3 37.6 %fusion.46 = f32[4096,3200]{1,0:T(8,128)} fusion(bf16[1,1024,3200]{2,1,0:T(8,128)(2,1)} %all-gather.13.cloned.1.call-done, bf16[1,4096,1024]{1,2,0:T(8,128)(2,1)} %copy.10, f32[4096]{0:T(1024)S(1)} %fusion.56), kind=kOutput, calls=%fused_computation.72 | convolution fusion | flops 26856128512 | bytes 67387392 | tf_op jit(solution)/shard_map/dot_general | solution.py:21
  97.8 10.1 all-gather.15.cloned.1.call-done
  107.9 58.0 %multiply_convert_fusion.1 = (bf16[4096,3200]{1,0:T(8,128)(2,1)}, f32[4096,3200]{1,0:T(8,128)}) fusion(f32[4096,3200]{1,0:T(8,128)} %fusion.46, bf16[1,1024,3200]{2,1,0:T(8,128)(2,1)} %all-gather.15.cloned.1.call-done, bf16[1,4096,1024]{1,2,0:T(8,128)(2,1)} %copy.10, f32[4096]{0:T(1024)S(1)} %fusion.56), kind=kOutput, calls=%fused_computation.13 | convolution fusion | flops 26934771712 | bytes 146030592 | tf_op jit(solution)/shard_map/dot_general | solution.py:22
  165.9 37.1 %fusion.18 = (f32[4096]{0:T(1024)S(1)}, bf16[4096,1024]{0,1:T(8,128)(2,1)}) fusion(bf16[4096,3200]{1,0:T(8,128)(2,1)} %get-tuple-element.20, bf16[1,3200,1024]{2,1,0:T(8,128)(2,1)} %all-gather.17.cloned.1.call-done, bf16[1,4096,1024]{1,2,0:T(8,128)(2,1)} %copy.10), kind=kOutput, calls=%fused_computation.40 | convolution fusion | flops 26864513024 | bytes 49561600 | tf_op jit(solution)/shard_map/dot_general | solution.py:10
  203.1 36.4 %convolution_convert_fusion.1 = bf16[4096,3200]{1,0:T(8,128)(2,1)} fusion(bf16[1,4096,1024]{2,1,0:T(8,128)(2,1)} %param.6, bf16[1,3200,1024]{2,1,0:T(8,128)(2,1)} %all-gather.21.cloned.1.call-done), kind=kOutput, calls=%fused_computation.21 | convolution fusion | flops 26856652800 | bytes 41156608 | tf_op jit(solution)/shard_map/transpose(jvp())/dot_general | solution.py:10
  239.4 11.6 %all-gather.23.cloned.1.call-done = bf16[1,1024,3200]{2,1,0:T(8,128)(2,1)} async-done(((bf16[1,256,3200]{2,1,0:T(8,128)(2,1)}), bf16[1,1024,3200]{2,1,0:T(8,128)(2,1)}) %all-gather.23.cloned.1.call-update) | async-done | bytes 6553616 | tf_op jit(solution)/shard_map/all_gather | solution.py:28
  251.0 37.7 %fusion.31 = f32[4096,3200]{1,0:T(8,128)} fusion(bf16[1,1024,3200]{2,1,0:T(8,128)(2,1)} %all-gather.23.cloned.1.call-done, bf16[4096,1024]{0,1:T(8,128)(2,1)} %get-tuple-element.23, f32[4096]{0:T(1024)S(1)} %fusion.57), kind=kOutput, calls=%fused_computation.57 | convolution fusion | flops 26856128512 | bytes 67387392 | tf_op jit(solution)/shard_map/jvp()/dot_general | solution.py:22
  288.6 10.4 all-gather.19.cloned.1.call-done
  299.0 69.3 %fusion.1 = (bf16[4096,3200]{1,0:T(8,128)(2,1)}, f32[4096,3200]{1,0:T(8,128)}) fusion(f32[4096,3200]{1,0:T(8,128)} %fusion.31, bf16[4096,3200]{1,0:T(8,128)(2,1)} %convolution_convert_fusion.1, bf16[1,1024,3200]{2,1,0:T(8,128)(2,1)} %all-gather.19.cloned.1.call-done, bf16[4096,1024]{0,1:T(8,128)(2,1)} %get-tuple-element.23, f32[4096]{0:T(1024)S(1)} %fusion.57), kind=kOutput, calls=%fused_computation.7 | convolution fusion | flops 27013414912 | bytes 172244992 | tf_op jit(solution)/shard_map/jvp()/dot_general | solution.py:21
  368.3 35.2 %fusion.35 = bf16[4096,1024]{0,1:T(8,128)(2,1)} fusion(bf16[4096,3200]{1,0:T(8,128)(2,1)} %get-tuple-element.24, bf16[1,1024,3200]{2,1,0:T(8,128)(2,1)} %all-gather.19.cloned.1.call-done), kind=kOutput, calls=%fused_computation.61 | convolution fusion | flops 26843545600 | bytes 41156608 | tf_op jit(solution)/shard_map/transpose(jvp())/dot_general | solution.py:21
  403.5 43.5 %fusion.20 = (f32[4096]{0:T(1024)S(1)}, bf16[4096,1024]{0,1:T(8,128)(2,1)}) fusion(bf16[4096,1024]{0,1:T(8,128)(2,1)S(1)} %copy-done.2, bf16[4096,1024]{0,1:T(8,128)(2,1)} %fusion.35, bf16[1,1024,3200]{2,1,0:T(8,128)(2,1)} %all-gather.23.cloned.1.call-done, bf16[4096,3200]{1,0:T(8,128)(2,1)} %convolution_convert_fusion.1, f32[4096,3200]{1,0:T(8,128)} %get-tuple-element.25), kind=kOutput, calls=%fused_computation.42 | convolution fusion | flops 26947350528 | bytes 110379008 | tf_op jit(solution)/shard_map/transpose(jvp())/dot_general | solution.py:22
  447.0 10.9 %fusion.23 = bf16[4096,1024]{0,1:T(8,128)(2,1)S(1)} fusion(bf16[4096,1024]{0,1:T(8,128)(2,1)} %get-tuple-element.23, bf16[4096,1024]{0,1:T(8,128)(2,1)} %get-tuple-element.27, bf16[1,4096,1024]{1,2,0:T(8,128)(2,1)} %copy.9, f32[4096]{0:T(1024)S(1)} %multiply_multiply_fusion.1, f32[4096]{0:T(1024)S(1)} %copy-done.11), kind=kLoop, calls=%fused_computation.45 | loop fusion | flops 29360128 | bytes 33587200 | tf_op jit(solution)/shard_map/transpose(jvp())/add_any | solution.py:14
  461.2 31.7 %convolution_convert_fusion.4 = bf16[3200,1024]{1,0:T(8,128)(2,1)} fusion(bf16[4096,3200]{1,0:T(8,128)(2,1)} %get-tuple-element.20, bf16[4096,1024]{0,1:T(8,128)(2,1)S(1)} %fusion.23), kind=kOutput, calls=%fused_computation.56 | convolution fusion | flops 26846822400 | bytes 41156608 | tf_op jit(solution)/shard_map/transpose(jvp())/dot_general | solution.py:10
  493.0 43.9 %fusion.26 = bf16[3200,1024]{1,0:T(8,128)(2,1)} fusion(bf16[1,4096,1024]{2,1,0:T(8,128)(2,1)} %param.6, f32[4096,3200]{1,0:T(8,128)} %fusion.31, f32[4096,3200]{1,0:T(8,128)} %get-tuple-element.25), kind=kOutput, calls=%fused_computation.51 | convolution fusion | flops 26925465600 | bytes 119799808 | tf_op jit(solution)/shard_map/transpose(jvp())/dot_general | solution.py:10
  537.0 68.5 %fusion.3 = (bf16[4096,3200]{1,0:T(8,128)(2,1)}, bf16[4096,3200]{1,0:T(8,128)(2,1)}) fusion(f32[4096,3200]{1,0:T(8,128)} %fusion.46, f32[4096,3200]{1,0:T(8,128)} %get-tuple-element.21, bf16[4096,1024]{0,1:T(8,128)(2,1)} %copy-done.1, bf16[1,3200,1024]{2,1,0:T(8,128)(2,1)} %all-gather.17.cloned.1.call-done), kind=kOutput, calls=%fused_computation.9 | convolution fusion | flops 27013939200 | bytes 172228608 | tf_op jit(solution)/shard_map/transpose(jvp())/dot_general | solution.py:10
  605.5 44.5 %fusion.29 = bf16[1024,3200]{1,0:T(8,128)(2,1)} fusion(bf16[4096,3200]{1,0:T(8,128)(2,1)} %get-tuple-element.29, bf16[1,4096,1024]{1,2,0:T(8,128)(2,1)} %copy.10, f32[4096]{0:T(1024)S(1)} %copy-done.7, f32[4096,3200]{1,0:T(8,128)} %fusion.46), kind=kOutput, calls=%fused_computation.52 | convolution fusion | flops 26938048512 | bytes 93601792 | tf_op jit(solution)/shard_map/transpose(jvp())/dot_general | solution.py:22
  650.1 44.1 %fusion.30 = bf16[1024,3200]{1,0:T(8,128)(2,1)} fusion(bf16[4096,3200]{1,0:T(8,128)(2,1)} %convolution_convert_fusion.1, bf16[4096,1024]{0,1:T(8,128)(2,1)} %get-tuple-element.23, f32[4096]{0:T(1024)S(1)} %copy-done.12, f32[4096,3200]{1,0:T(8,128)} %get-tuple-element.25), kind=kOutput, calls=%fused_computation.53 | convolution fusion | flops 26938048512 | bytes 93601792 | tf_op jit(solution)/shard_map/transpose(jvp())/dot_general | solution.py:22
  694.4 37.0 %convolution_convert_fusion.2 = bf16[1024,3200]{1,0:T(8,128)(2,1)} fusion(bf16[4096,3200]{1,0:T(8,128)(2,1)} %get-tuple-element.24, bf16[4096,1024]{0,1:T(8,128)(2,1)} %get-tuple-element.23, f32[4096]{0:T(1024)S(1)} %copy-done.12), kind=kOutput, calls=%fused_computation.54 | convolution fusion | flops 26856128512 | bytes 41172992 | tf_op jit(solution)/shard_map/transpose(jvp())/dot_general | solution.py:21
  731.5 37.0 %convolution_convert_fusion.3 = bf16[1024,3200]{1,0:T(8,128)(2,1)} fusion(bf16[4096,3200]{1,0:T(8,128)(2,1)} %get-tuple-element.28, bf16[1,4096,1024]{1,2,0:T(8,128)(2,1)} %copy.10, f32[4096]{0:T(1024)S(1)} %copy-done.8), kind=kOutput, calls=%fused_computation.55 | convolution fusion | flops 26856128512 | bytes 41172992 | tf_op jit(solution)/shard_map/transpose(jvp())/dot_general | solution.py:21
  768.5 35.2 %fusion.44 = bf16[4096,1024]{0,1:T(8,128)(2,1)} fusion(bf16[4096,3200]{1,0:T(8,128)(2,1)} %get-tuple-element.28, bf16[1,1024,3200]{2,1,0:T(8,128)(2,1)} %all-gather.13.cloned.1.call-done), kind=kOutput, calls=%fused_computation.70 | convolution fusion | flops 26843545600 | bytes 41156608 | tf_op jit(solution)/shard_map/transpose(jvp())/dot_general | solution.py:21
  803.8 15.7 %reduce-scatter.9.cloned.1.call-done = bf16[256,3200]{1,0:T(8,128)(2,1)} async-done(((bf16[1024,3200]{1,0:T(8,128)(2,1)}), bf16[256,3200]{1,0:T(8,128)(2,1)}) %reduce-scatter.9.cloned.1.call-update) | async-done | bytes 1638416 | tf_op jit(solution)/shard_map/reduce_scatter | solution.py:31
  819.5 57.2 %reduce-scatter.7.cloned.1.call-done = bf16[256,3200]{1,0:T(8,128)(2,1)} async-done(((bf16[1024,3200]{1,0:T(8,128)(2,1)}), bf16[256,3200]{1,0:T(8,128)(2,1)}) %reduce-scatter.7.cloned.1.call-update) | async-done | bytes 1638416 | tf_op jit(solution)/shard_map/reduce_scatter | solution.py:31
  876.7 43.6 %fusion.17 = (f32[4096]{0:T(1024)S(1)}, bf16[4096,1024]{0,1:T(8,128)(2,1)}) fusion(bf16[1,4096,1024]{1,2,0:T(8,128)(2,1)} %copy.10, bf16[4096,1024]{0,1:T(8,128)(2,1)} %fusion.44, bf16[1,1024,3200]{2,1,0:T(8,128)(2,1)} %all-gather.15.cloned.1.call-done, bf16[4096,3200]{1,0:T(8,128)(2,1)} %get-tuple-element.29, f32[4096,3200]{1,0:T(8,128)} %fusion.46), kind=kOutput, calls=%fused_computation.39 | convolution fusion | flops 26947350528 | bytes 110379008 | tf_op jit(solution)/shard_map/transpose(jvp())/dot_general | solution.py:22
  920.3 12.1 %fusion.22 = bf16[1,4096,1024]{1,2,0:T(8,128)(2,1)} fusion(bf16[4096,1024]{0,1:T(8,128)(2,1)} %copy-done.1, bf16[4096,1024]{0,1:T(8,128)(2,1)} %get-tuple-element.31, bf16[1,4096,1024]{1,2,0:T(8,128)(2,1)S(1)} %copy-done, f32[4096]{0:T(1024)S(1)} %multiply_multiply_fusion, f32[4096]{0:T(1024)S(1)} %copy-done.9), kind=kLoop, calls=%fused_computation.44 | loop fusion | flops 29360128 | bytes 33587200 | tf_op jit(solution)/shard_map/broadcast_in_dim | solution.py:44
  932.5 11.9 %copy.11 = bf16[1,4096,1024]{2,1,0:T(8,128)(2,1)} copy(bf16[1,4096,1024]{1,2,0:T(8,128)(2,1)} %fusion.22) | data formatting | bytes 16777216
  944.4 124.0 %all-reduce.3.cloned.1.call-done = (bf16[1,256,3200]{2,1,0:T(8,128)(2,1)}, bf16[1,256,3200]{2,1,0:T(8,128)(2,1)}, bf16[1,256,3200]{2,1,0:T(8,128)(2,1)}, bf16[1,...) async-done(((bf16[1,256,3200]{2,1,0:T(8,128)(2,1)}, bf16[1,256,3200]{2,1,0:T(8,128)(2,1)}, bf16[1,256,3200]{2,1,0:T(8,128)(2,1)}, ...) | async-done | bytes 9830416 | tf_op jit(solution)/shard_map/psum | solution.py:31
  1072.3 5.0 pad_maximum_fusion
  (69 shorter events, 16.2 us)
Async XLA Ops:
  7.2 8.1 copy-start.3
  7.2 53.1 %all-gather.13.cloned.1.call-start = ((), (), s32[]{:S(2)}) async-start(), calls=%async_computation.12 | async-start | bytes 8192000 | tf_op jit(solution)/shard_map/all_gather | solution.py:28
  11.2 96.6 %all-gather.15.cloned.1.call-start = ((), (), s32[]{:S(2)}) async-start(), calls=%async_computation.13 | async-start | bytes 8192000 | tf_op jit(solution)/shard_map/all_gather | solution.py:28
  15.2 150.7 %all-gather.17.cloned.1.call-start = ((), (), s32[]{:S(2)}) async-start(), calls=%async_computation.14 | async-start | bytes 8192000 | tf_op jit(solution)/shard_map/all_gather | solution.py:28
  17.4 185.7 %all-gather.21.cloned.1.call-start = ((), (), s32[]{:S(2)}) async-start(), calls=%async_computation.16 | async-start | bytes 8192000 | tf_op jit(solution)/shard_map/all_gather | solution.py:28
  17.9 233.0 %all-gather.23.cloned.1.call-start = ((), (), s32[]{:S(2)}) async-start(), calls=%async_computation.17 | async-start | bytes 8192000 | tf_op jit(solution)/shard_map/all_gather | solution.py:28
  18.5 280.5 %all-gather.19.cloned.1.call-start = ((), (), s32[]{:S(2)}) async-start(), calls=%async_computation.15 | async-start | bytes 8192000 | tf_op jit(solution)/shard_map/all_gather | solution.py:28
  19.1 784.6 %reduce-scatter.15.cloned.1.call-start = ((), (), s32[]{:S(2)}) async-start(), calls=%async_computation.10 | async-start | bytes 8192000 | tf_op jit(solution)/shard_map/reduce_scatter | solution.py:31
  36.1 0.6 copy-start.4
  36.8 71.1 %copy-start.6 = (f32[4096]{0:T(1024)}, f32[4096]{0:T(1024)S(1)}, u32[]{:S(2)}) copy-start(f32[4096]{0:T(1024)S(1)} %fusion.56) | copy-start | bytes 49156
  203.0 36.4 %copy-start.13 = (f32[4096]{0:T(1024)}, f32[4096]{0:T(1024)S(1)}, u32[]{:S(2)}) copy-start(f32[4096]{0:T(1024)S(1)} %get-tuple-element.22) | copy-start | bytes 49156
  203.0 96.0 %copy-start.10 = (f32[4096]{0:T(1024)}, f32[4096]{0:T(1024)S(1)}, u32[]{:S(2)}) copy-start(f32[4096]{0:T(1024)S(1)} %fusion.57) | copy-start | bytes 49156
  368.3 35.2 %copy-start.2 = (bf16[4096,1024]{0,1:T(8,128)(2,1)S(1)}, bf16[4096,1024]{0,1:T(8,128)(2,1)}, u32[]{:S(2)}) copy-start(bf16[4096,1024]{0,1:T(8,128)(2,1)} %get-tuple-element.23) | copy-start | bytes 25165828
  403.5 43.5 %copy-start.14 = (f32[4096]{0:T(1024)S(1)}, f32[4096]{0:T(1024)}, u32[]{:S(2)}) copy-start(f32[4096]{0:T(1024)} %copy-done.13) | copy-start | bytes 49156
  403.5 43.5 %copy-start.11 = (f32[4096]{0:T(1024)S(1)}, f32[4096]{0:T(1024)}, u32[]{:S(2)}) copy-start(f32[4096]{0:T(1024)} %copy-done.10) | copy-start | bytes 49156
  457.9 3.3 copy-start.1
  493.0 310.8 %reduce-scatter.17.cloned.1.call-start = ((), (), s32[]{:S(2)}) async-start(), calls=%async_computation.11 | async-start | bytes 8192000 | tf_op jit(solution)/shard_map/reduce_scatter | solution.py:31
  537.0 266.8 %reduce-scatter.11.cloned.1.call-start = ((), (), s32[]{:S(2)}) async-start(), calls=%async_computation.8 | async-start | bytes 8192000 | tf_op jit(solution)/shard_map/reduce_scatter | solution.py:31
  537.0 68.5 %copy-start.7 = (f32[4096]{0:T(1024)S(1)}, f32[4096]{0:T(1024)}, u32[]{:S(2)}) copy-start(f32[4096]{0:T(1024)} %copy-done.6) | copy-start | bytes 49156
  605.5 44.6 %copy-start.12 = (f32[4096]{0:T(1024)S(1)}, f32[4096]{0:T(1024)}, u32[]{:S(2)}) copy-start(f32[4096]{0:T(1024)} %copy-done.10) | copy-start | bytes 49156
  650.1 153.7 %reduce-scatter.13.cloned.1.call-start = ((), (), s32[]{:S(2)}) async-start(), calls=%async_computation.9 | async-start | bytes 8192000 | tf_op jit(solution)/shard_map/reduce_scatter | solution.py:31
  694.3 37.1 %copy-start.8 = (f32[4096]{0:T(1024)S(1)}, f32[4096]{0:T(1024)}, u32[]{:S(2)}) copy-start(f32[4096]{0:T(1024)} %copy-done.6) | copy-start | bytes 49156
  694.3 125.2 %reduce-scatter.9.cloned.1.call-start = ((), (), s32[]{:S(2)}) async-start(), calls=%async_computation.7 | async-start | bytes 8192000 | tf_op jit(solution)/shard_map/reduce_scatter | solution.py:31
  731.4 145.3 %reduce-scatter.7.cloned.1.call-start = ((), (), s32[]{:S(2)}) async-start(), calls=%async_computation.6 | async-start | bytes 8192000 | tf_op jit(solution)/shard_map/reduce_scatter | solution.py:31
  768.5 299.9 %all-reduce.3.cloned.1.call-start = ((), (), s32[]{:S(2)}) async-start(), calls=%async_computation.18 | async-start | bytes 19660800 | tf_op jit(solution)/shard_map/psum | solution.py:31
  876.7 43.6 %copy-start.5 = (f32[4096]{0:T(1024)S(1)}, f32[4096]{0:T(1024)}, u32[]{:S(2)}) copy-start(f32[4096]{0:T(1024)} %copy-done.4) | copy-start | bytes 49156
  876.7 43.6 %copy-start = (bf16[1,4096,1024]{1,2,0:T(8,128)(2,1)S(1)}, bf16[1,4096,1024]{1,2,0:T(8,128)(2,1)}, u32[]{:S(2)}) copy-start(bf16[1,4096,1024]{1,2,0:T(8,128)(2,1)} %copy.10) | copy-start | bytes 25165828
  876.7 43.6 %copy-start.9 = (f32[4096]{0:T(1024)S(1)}, f32[4096]{0:T(1024)}, u32[]{:S(2)}) copy-start(f32[4096]{0:T(1024)} %copy-done.6) | copy-start | bytes 49156
Sparse Core Ops, SparseCore 0:
  11.4 48.8 all-gather.12
  61.8 46.0 all-gather.14
  109.4 46.0 all-gather.16
  156.9 46.0 all-gather.20
  204.9 46.0 all-gather.22
  252.9 46.0 all-gather.18
  493.1 54.7 reduce-scatter.14
  550.4 54.7 reduce-scatter.16
  650.2 54.7 reduce-scatter.10
  707.4 54.7 reduce-scatter.12
  764.7 54.7 reduce-scatter.8
  821.9 54.7 reduce-scatter.6
  881.4 186.9 all-reduce.2
where the time goes:
time: 1090 us; the launch traced here: 1080 us
  matrix products  740 us (68%)
  waiting for transfers between devices  243 us (22%)
  local copies, waits for them, and re-layouts  49.3 us (5%)
  other arithmetic  37.1 us (3%)
  between operations  14.3 us (1%)
    dot_general x6, matrix products, layer(): up = jnp.dot(a, w['w_up'], preferred_element_type=jnp.float32)  271 us
    dot_general x6, matrix products, layer(): gate = jnp.dot(a, w['w_gate'], preferred_element_type=jnp.float32)  251 us
    dot_general x5, matrix products, matmul(): jnp.dot(a, w, preferred_element_type=jnp.float32).astype(jnp.bfloat16)  218 us
    psum x1, waiting for transfers between devices, summed(): lax.psum(lax.psum_scatter(term, 's', scatter_dimension=0, tiled=True), 'r')  124 us
    reduce_scatter x6, waiting for transfers between devices, summed(): lax.psum_scatter(term, 's', scatter_dimension=0, tiled=True)  72.9 us
    all_gather x6, waiting for transfers between devices, fetched(): lax.all_gather(w[number], 's', axis=0, tiled=True)  43.9 us
    unnamed x33, local copies, waits for them, and re-layouts  39.3 us
  transfers between devices with their start and end apart: 13, of which 7 were waited for; matrix products, arithmetic and copies ran while one was open for 57% of the time, Pallas kernels for 0%

commit v1 on v0

v1 whole, which is shorter than its diff:
```python
import functools

import jax
import jax.numpy as jnp
from jax import lax
from jax.experimental import pallas as pl
from jax.experimental.pallas import tpu as pltpu
from jax.sharding import PartitionSpec as P

BF, F32 = jnp.bfloat16, jnp.float32
MESH = pl.DeviceIdType.MESH
NT = (((1,), (1,)), ((), ()))
TN = (((0,), (0,)), ((), ()))
ANY = pl.BlockSpec(memory_space=pl.ANY)
CHUNKS = 5
VMEM_LIMIT = 67043328


def dot(a, b, dims=(((1,), (0,)), ((), ()))):
    return lax.dot_general(a, b, dims, preferred_element_type=F32)


def scale_of(wide):
    return lax.rsqrt(jnp.mean(wide * wide, -1, keepdims=True) + 1e-6)


def pieces(width):
    first = 256 if width > 512 else width // 2
    return ((0, first), (first, width - first))


def rows(start, size, unit=16):
    return pl.ds(pl.multiple_of(start, unit) if size % unit == 0 else start, size)


def gate_up_kernel(x_ref, wg_ref, wu_ref, a_ref, hid_ref, g_ref, u_ref):
    wide = x_ref[...].astype(F32)
    a = (wide * scale_of(wide)).astype(BF)
    a_ref[...] = a
    width = wg_ref.shape[1] // CHUNKS
    for j in range(CHUNKS):
        c = pl.ds(j * width, width)
        both = dot(a, jnp.concatenate([wg_ref[:, c], wu_ref[:, c]], 1))
        g, u = both[:, :width], both[:, width:]
        g_ref[:, c], u_ref[:, c] = g, u
        hid_ref[:, c] = (g * jax.nn.sigmoid(g) * u).astype(BF)


def gate_up(x, wg, wu):
    t, d = x.shape
    f = wg.shape[1]
    tm = t // 16
    whole = pl.BlockSpec((d, f), lambda i: (0, 0), pipeline_mode=pl.Buffered(1))
    part = lambda n: pl.BlockSpec((tm, n), lambda i: (i, 0))
    return pl.pallas_call(
        gate_up_kernel,
        grid=(t // tm,),
        in_specs=[part(d), whole, whole],
        out_specs=[part(d), part(f), part(f), part(f)],
        out_shape=[jax.ShapeDtypeStruct((t, n), k) for n, k in ((d, BF), (f, BF), (f, F32), (f, F32))],
        compiler_params=pltpu.CompilerParams(vmem_limit_bytes=VMEM_LIMIT, dimension_semantics=("arbitrary",)),
        cost_estimate=pl.CostEstimate(flops=4 * t * d * f, bytes_accessed=12 * t * f, transcendentals=t * f),
        name="gate_up",
    )(x, wg, wu)


def down_kernel(hid_ref, w_ref, x_ref, h_ref, a_ref):
    h = (x_ref[...].astype(F32) + dot(hid_ref[...], w_ref[...]).astype(BF).astype(F32)).astype(BF)
    h_ref[...] = h
    wide = h.astype(F32)
    a_ref[...] = (wide * scale_of(wide)).astype(BF)


def down(hid, w, x):
    t, d = x.shape
    f = w.shape[0]
    tm = t // 8
    part = lambda n: pl.BlockSpec((tm, n), lambda i: (i, 0))
    return pl.pallas_call(
        down_kernel,
        grid=(t // tm,),
        in_specs=[part(f), pl.BlockSpec((f, d), lambda i: (0, 0), pipeline_mode=pl.Buffered(1)), part(d)],
        out_specs=[part(d), part(d)],
        out_shape=[jax.ShapeDtypeStruct((t, d), BF)] * 2,
        compiler_params=pltpu.CompilerParams(vmem_limit_bytes=VMEM_LIMIT, dimension_semantics=("arbitrary",)),
        cost_estimate=pl.CostEstimate(flops=2 * t * d * f, bytes_accessed=2 * t * f, transcendentals=0),
        name="down",
    )(hid, w, x)


def here():
    s = lax.axis_index("s")
    return lax.axis_index("r"), lax.div(s, 2), lax.rem(s, 2)


def send(src, dst, sems, to):
    return pltpu.make_async_remote_copy(
        src_ref=src, dst_ref=dst, send_sem=sems[0], recv_sem=sems[1], device_id=to, device_id_type=MESH
    )


def start(copies):
    for copy in copies:
        copy.start()


def wait(copies):
    for copy in copies:
        copy.wait()


def backward_kernel(saved, *refs):
    n_in = 8 if saved else 6
    a_hbm, h_hbm, dy_hbm, wg_hbm, wu_hbm, wd_hbm = refs[:6]
    g_hbm, u_hbm = refs[6:n_in] if saved else (None, None)
    out_hbm, og_hbm, ou_hbm, od_hbm, dgu_hbm, dwd_hbm = refs[n_in : n_in + 6]
    (stg, buf_d, acc, buf_x, s_x, s_r, buf_r, s_g, sem_d, sem_x, sem_r, sem_g, sem_gl, free_d, free_x, free_r, entered) = refs[n_in + 6 :]

    t, d = a_hbm.shape
    f = wd_hbm.shape[0]
    c = f // CHUNKS
    own = d // 4
    quarter = own // 4
    own_d = f // 4
    rd = own_d // 5
    qd = d // 4
    me_r, x, core = here()
    partner = {"s": x * 2 + (1 - core)}
    across = {"s": (1 - x) * 2 + core}
    peers = [(lax.rem(me_r + k, 4), {"r": lax.rem(me_r + k, 4)}) for k in (1, 2, 3)]
    everyone = [partner, across] + [p for _, p in peers]

    barrier = pltpu.get_barrier_semaphore()
    for p in everyone:
        pl.semaphore_signal(barrier, inc=1, device_id=p, device_id_type=MESH)
    pl.semaphore_wait(barrier, 5)

    def d_copies():
        return [
            send(stg.at[rows((2 * k + 1 - core) * own, own), :], buf_d.at[k], (sem_d.at[0, k], sem_d.at[1, k]), partner)
            for k in range(2)
        ]

    def x_copies():
        return [send(s_x, buf_x, (sem_x.at[0], sem_x.at[1]), across)]

    def r_copies():
        return [
            send(s_r.at[rows(n * quarter, quarter), :], buf_r.at[k], (sem_r.at[0, k], sem_r.at[1, k]), p)
            for k, (n, p) in enumerate(peers)
        ]

    def g_copies(p):
        at = (rows(me_r * quarter, quarter), rows(p * c, c, 128))
        far = [
            send(s_g.at[:, pl.ds(i * c, c)], o.at[at], (sem_g.at[0, lax.rem(p, 2), i, k], sem_g.at[1, lax.rem(p, 2), i, k]), to)
            for k, (_, to) in enumerate(peers)
            for i, o in enumerate((og_hbm, ou_hbm))
        ]
        near = [pltpu.make_async_copy(s_g.at[:, pl.ds(i * c, c)], o.at[at], sem_gl.at[i]) for i, o in enumerate((og_hbm, ou_hbm))]
        return far + near

    def e0(p, first):
        if not first:
            pl.semaphore_wait(free_d, 1)
        start(d_copies())

    def e1(p, first, last):
        wait(d_copies())
        acc[lax.rem(p, 2)] = stg[rows((2 * x + core) * own, own), :].astype(F32) + buf_d[x].astype(F32)
        s_x[...] = (stg[rows((2 * (1 - x) + core) * own, own), :].astype(F32) + buf_d[1 - x].astype(F32)).astype(BF)
        if not last:
            pl.semaphore_signal(free_d, inc=1, device_id=partner, device_id_type=MESH)
        if not first:
            pl.semaphore_wait(free_x, 1)
        start(x_copies())

    def e2(p, first, last):
        wait(x_copies())
        total = acc[lax.rem(p, 2)] + buf_x[...].astype(F32)
        acc[lax.rem(p, 2)] = total
        s_r[...] = total.astype(BF)
        if not last:
            pl.semaphore_signal(free_x, inc=1, device_id=across, device_id_type=MESH)
        if not first:
            for k in range(3):
                pl.semaphore_wait(free_r.at[k], 1)
        start(r_copies())

    def e3(p, last):
        wait(r_copies())
        total = acc[lax.rem(p, 2), rows(me_r * quarter, quarter), :]
        for k in range(3):
            total = total + buf_r[k].astype(F32)
        s_g[...] = total.astype(BF)
        if not last:
            for k, (_, to) in enumerate(peers):
                pl.semaphore_signal(free_r.at[2 - k], inc=1, device_id=to, device_id_type=MESH)
        start(g_copies(p))

    def e4(p):
        wait(g_copies(p))

    tm = t // 8 if saved else t // 4
    tiles = t // tm

    def chunks(*bufs):
        if saved:
            a_v, dy_v, wd_v, hid_v, dgs, dst, g_v, u_v, sem_a, sem_w, sem_o, sem_s = bufs
        else:
            a_v, dy_v, wd_v, hid_v, dgs, dst, wgu_v, sem_a, sem_w, sem_o = bufs

        def a_copies(i):
            at = rows(i * tm, tm)
            return [
                pltpu.make_async_copy(a_hbm.at[at, :], a_v.at[at, :], sem_a.at[0, i]),
                pltpu.make_async_copy(dy_hbm.at[at, :], dy_v.at[at, :], sem_a.at[1, i]),
            ]

        def w_copies(j):
            slot = lax.rem(j, 2)
            at = rows(j * c, c, 128)
            w = [pltpu.make_async_copy(wd_hbm.at[at, :], wd_v.at[slot], sem_w.at[slot, 0])]
            if not saved:
                w.append(pltpu.make_async_copy(wg_hbm.at[:, at], wgu_v.at[slot, :, pl.ds(0, c)], sem_w.at[slot, 1]))
                w.append(pltpu.make_async_copy(wu_hbm.at[:, at], wgu_v.at[slot, :, pl.ds(c, c)], sem_w.at[slot, 2]))
            return w

        def s_copies(n):
            slot = lax.rem(n, 2)
            at = (rows(lax.rem(n, tiles) * tm, tm), rows(lax.div(n, tiles) * c, c, 128))
            return [
                pltpu.make_async_copy(g_hbm.at[at], g_v.at[slot], sem_s.at[slot, 0]),
                pltpu.make_async_copy(u_hbm.at[at], u_v.at[slot], sem_s.at[slot, 1]),
            ]

        def o_copies(j):
            return [
                pltpu.make_async_copy(dgs.at[:, pl.ds(0, c)], dgu_hbm.at[:, rows(j * c, c, 128)], sem_o.at[0]),
                pltpu.make_async_copy(dgs.at[:, pl.ds(c, c)], dgu_hbm.at[:, rows(f + j * c, c, 128)], sem_o.at[1]),
            ]

        def dw_copy(j):
            return [pltpu.make_async_copy(dst, dwd_hbm.at[rows(j * c, c), :], sem_o.at[2])]

        start(w_copies(0))
        if saved:
            start(s_copies(0))
        for i in range(tiles):
            start(a_copies(i))

        def chunk(j, _):
            slot = lax.rem(j, 2)

            @pl.when(j >= 3)
            def _():
                e4(j - 3)

            @pl.when(j == 2)
            def _():
                e2(j - 2, True, False)

            @pl.when(j >= 3)
            def _():
                e2(j - 2, False, False)

            @pl.when(j == 1)
            def _():
                e0(j - 1, True)

            @pl.when(j >= 2)
            def _():
                e0(j - 1, False)

            @pl.when(j >= 1)
            def _():
                wait(o_copies(j - 1))

            wait(w_copies(j))

            @pl.when(j + 1 < CHUNKS)
            def _():
                start(w_copies(j + 1))

            def tile(i, _):
                @pl.when(j == 0)
                def _():
                    wait(a_copies(i))

                if saved:
                    n = j * tiles + i

                    @pl.when(n + 1 < CHUNKS * tiles)
                    def _():
                        start(s_copies(n + 1))

                    wait(s_copies(n))

                @pl.when(jnp.logical_and(i == tiles // 2, j == 1))
                def _():
                    e1(j - 1, True, False)

                @pl.when(jnp.logical_and(i == tiles // 2, j >= 2))
                def _():
                    e1(j - 1, False, False)

                r = rows(i * tm, tm)
                for p0, w in pieces(c):
                    if saved:
                        g = g_v[lax.rem(n, 2), :, pl.ds(p0, w)]
                        u = u_v[lax.rem(n, 2), :, pl.ds(p0, w)]
                    else:
                        a = a_v[r, :]
                        both = dot(a, jnp.concatenate([wgu_v[slot, :, pl.ds(p0, w)], wgu_v[slot, :, pl.ds(c + p0, w)]], 1))
                        g, u = both[:, :w], both[:, w:]
                    dh = dot(dy_v[r, :], wd_v[slot, pl.ds(p0, w), :], NT).astype(BF).astype(F32)
                    s = jax.nn.sigmoid(g)
                    silu = g * s
                    hid_v[r, pl.ds(p0, w)] = (silu * u).astype(BF)
                    dgs[r, pl.ds(c + p0, w)] = (dh * silu).astype(BF)
                    dgs[r, pl.ds(p0, w)] = (dh * u * (s + silu * (1.0 - s))).astype(BF)
                return 0

            lax.fori_loop(0, tiles, tile, 0)
            start(o_copies(j))

            @pl.when(j >= 1)
            def _():
                wait(dw_copy(j - 1))

            for p0, w in pieces(c):
                dst[pl.ds(p0, w), :] = dot(hid_v[:, pl.ds(p0, w)], dy_v[...], TN).astype(BF)
            start(dw_copy(j))

            @pl.when(j >= 2)
            def _():
                e3(j - 2, False)

            for k in range(2):
                stg[pl.ds(k * (d // 2), d // 2), :] = dot(a_v[:, pl.ds(k * (d // 2), d // 2)], dgs[...], TN).astype(BF)
            return 0

        lax.fori_loop(0, CHUNKS, chunk, 0)
        wait(o_copies(CHUNKS - 1))
        wait(dw_copy(CHUNKS - 1))

    bufs = [
        pltpu.VMEM((t, d), BF),
        pltpu.VMEM((t, d), BF),
        pltpu.VMEM((2, c, d), BF),
        pltpu.VMEM((t, c), BF),
        pltpu.VMEM((t, 2 * c), BF),
        pltpu.VMEM((c, d), BF),
    ]
    bufs += [pltpu.VMEM((2, tm, c), F32)] * 2 if saved else [pltpu.VMEM((2, d, 2 * c), BF)]
    bufs += [pltpu.SemaphoreType.DMA((2, tiles)), pltpu.SemaphoreType.DMA((2, 3)), pltpu.SemaphoreType.DMA((3,))]
    bufs += [pltpu.SemaphoreType.DMA((2, 2))] if saved else []
    pl.run_scoped(chunks, *bufs)

    ta = t // 8

    def last(wg_v, wu_v, dgu_v, h_v, dy_v, o_v, own_v, bd_v, ac_v, bx_v, sx_v, br_v, sg_v, sem_w, sem_i, sem_o, dd, dx, dr, dg, dl):
        def i_copies(i):
            slot = lax.rem(i, 2)
            at = rows(i * ta, ta)
            return [
                pltpu.make_async_copy(dgu_hbm.at[at, :], dgu_v.at[slot], sem_i.at[slot, 0]),
                pltpu.make_async_copy(h_hbm.at[at, :], h_v.at[slot], sem_i.at[slot, 1]),
                pltpu.make_async_copy(dy_hbm.at[at, :], dy_v.at[slot], sem_i.at[slot, 2]),
            ]

        def o_copy(i):
            slot = lax.rem(i, 2)
            return [pltpu.make_async_copy(o_v.at[slot], out_hbm.at[rows(i * ta, ta), :], sem_o.at[slot])]

        def w_copy(k):
            return [pltpu.make_async_copy((wg_hbm, wu_hbm)[k], (wg_v, wu_v)[k], sem_w.at[k])]

        def dd_copies(k):
            far = [
                send(
                    dwd_hbm.at[rows((2 * m + 1 - core) * own_d + k * rd, rd), :],
                    bd_v.at[k, m],
                    (dd.at[0, k, m], dd.at[1, k, m]),
                    partner,
                )
                for m in range(2)
            ]
            near = [
                pltpu.make_async_copy(dwd_hbm.at[rows((2 * m + core) * own_d + k * rd, rd), :], own_v.at[k, m], dl.at[0, k, m])
                for m in range(2)
            ]
            return far + near

        def dx_copies(k):
            return [send(sx_v.at[k], bx_v.at[k], (dx.at[0, k], dx.at[1, k]), across)]

        def dr_copies(k):
            return [
                send(sx_v.at[k, :, rows(n * qd, qd, 128)], br_v.at[k, m], (dr.at[0, k, m], dr.at[1, k, m]), to)
                for m, (n, to) in enumerate(peers)
            ]

        def dg_copies(k):
            at = (rows(k * rd, rd), rows(me_r * qd, qd, 128))
            far = [send(sg_v.at[k], od_hbm.at[at], (dg.at[0, k, m], dg.at[1, k, m]), to) for m, (_, to) in enumerate(peers)]
            return far + [pltpu.make_async_copy(sg_v.at[k], od_hbm.at[at], dl.at[1, k, 0])]

        def f0(k):
            start(dd_copies(k))

        def f1(k):
            wait(dd_copies(k))
            ac_v[k] = own_v[k, x].astype(F32) + bd_v[k, x].astype(F32)
            sx_v[k] = (own_v[k, 1 - x].astype(F32) + bd_v[k, 1 - x].astype(F32)).astype(BF)
            start(dx_copies(k))

        def f2(k):
            wait(dx_copies(k))
            total = ac_v[k] + bx_v[k].astype(F32)
            ac_v[k] = total
            sx_v[k] = total.astype(BF)
            start(dr_copies(k))

        def f3(k):
            wait(dr_copies(k))
            total = ac_v[k, :, rows(me_r * qd, qd, 128)]
            for m in range(3):
                total = total + br_v[k, m].astype(F32)
            sg_v[k] = total.astype(BF)
            start(dg_copies(k))

        def f4(k):
            wait(dg_copies(k))

        end = CHUNKS - 1
        todo = {
            0: [lambda: e4(end - 2), lambda: e2(end - 1, False, False), lambda: e0(end, False)],
            1: [lambda: e1(end, False, True)],
            2: [lambda: f1(0), lambda: f1(1)],
            3: [lambda: e3(end - 1, False), lambda: f1(2)],
            4: [lambda: f1(3), lambda: f1(4)],
            5: [lambda: e2(end, False, True)],
            6: [lambda: e4(end - 1)],
            7: [lambda: f2(0)],
            8: [lambda: e3(end, True)],
            9: [lambda: f2(1), lambda: f3(0)],
            11: [lambda: f2(2), lambda: f3(1)],
            12: [lambda: e4(end)],
            13: [lambda: f2(3), lambda: f3(2)],
            15: [lambda: f2(4), lambda: f3(3)],
        }

        def events(i, half):
            for point, does in todo.items():
                if point % 2 == half:

                    @pl.when(i == point // 2)
                    def _(does=does):
                        for do in does:
                            do()

        start(w_copy(0))
        start(i_copies(0))
        start(w_copy(1))
        for p in everyone:
            pl.semaphore_signal(entered, inc=1, device_id=p, device_id_type=MESH)
        pl.semaphore_wait(entered, 5)
        for k in range(5):
            f0(k)

        def tile(i, _):
            slot = lax.rem(i, 2)

            @pl.when(i + 1 < 8)
            def _():
                start(i_copies(i + 1))

            events(i, 0)
            wait(i_copies(i))

            @pl.when(i == 0)
            def _():
                wait(w_copy(0))

            by_g = dot(dgu_v[slot, :, pl.ds(0, f)], wg_v[...], NT).astype(BF)
            o_v[slot] = by_g
            events(i, 1)

            @pl.when(i == 0)
            def _():
                wait(w_copy(1))

            by_u = dot(dgu_v[slot, :, pl.ds(f, f)], wu_v[...], NT).astype(BF)
            by_a = (o_v[slot].astype(F32) + by_u.astype(F32)).astype(BF).astype(F32)
            wide = h_v[slot].astype(F32)
            scale = scale_of(wide)
            by_scale = jnp.sum(by_a * wide, -1, keepdims=True)
            by_wide = (by_a * scale - (by_scale * scale * scale * scale * (1.0 / d)) * wide).astype(BF)
            o_v[slot] = (dy_v[slot].astype(F32) + by_wide.astype(F32)).astype(BF)
            start(o_copy(i))

            @pl.when(i >= 1)
            def _():
                wait(o_copy(i - 1))

            return 0

        lax.fori_loop(0, 8, tile, 0)
        wait(o_copy(7))
        f3(4)
        for k in range(5):
            f4(k)

    pl.run_scoped(
        last,
        pltpu.VMEM((d, f), BF),
        pltpu.VMEM((d, f), BF),
        pltpu.VMEM((2, ta, 2 * f), BF),
        pltpu.VMEM((2, ta, d), BF),
        pltpu.VMEM((2, ta, d), BF),
        pltpu.VMEM((2, ta, d), BF),
        pltpu.VMEM((5, 2, rd, d), BF),
        pltpu.VMEM((5, 2, rd, d), BF),
        pltpu.VMEM((5, rd, d), F32),
        pltpu.VMEM((5, rd, d), BF),
        pltpu.VMEM((5, rd, d), BF),
        pltpu.VMEM((5, 3, rd, qd), BF),
        pltpu.VMEM((5, rd, qd), BF),
        pltpu.SemaphoreType.DMA((2,)),
        pltpu.SemaphoreType.DMA((2, 3)),
        pltpu.SemaphoreType.DMA((2,)),
        pltpu.SemaphoreType.DMA((2, 5, 2)),
        pltpu.SemaphoreType.DMA((2, 5)),
        pltpu.SemaphoreType.DMA((2, 5, 3)),
        pltpu.SemaphoreType.DMA((2, 5, 3)),
        pltpu.SemaphoreType.DMA((2, 5, 2)),
    )


def backward(a, h, dy, wg, wu, wd, saved, number):
    t, d = a.shape
    f = wd.shape[0]
    c = f // CHUNKS
    own, dma = d // 4, pltpu.SemaphoreType.DMA
    shapes = [(t, d), (own, f), (own, f), (f // 4, d), (t, 2 * f), (f, d)]
    out = pl.pallas_call(
        functools.partial(backward_kernel, saved is not None),
        in_specs=[ANY] * (8 if saved is not None else 6),
        out_specs=[ANY] * len(shapes),
        out_shape=[jax.ShapeDtypeStruct(s, BF) for s in shapes],
        scratch_shapes=[
            pltpu.VMEM((d, 2 * c), BF),
            pltpu.VMEM((2, own, 2 * c), BF),
            pltpu.VMEM((2, own, 2 * c), F32),
            pltpu.VMEM((own, 2 * c), BF),
            pltpu.VMEM((own, 2 * c), BF),
            pltpu.VMEM((own, 2 * c), BF),
            pltpu.VMEM((3, own // 4, 2 * c), BF),
            pltpu.VMEM((own // 4, 2 * c), BF),
            dma((2, 2)),
            dma((2,)),
            dma((2, 3)),
            dma((2, 2, 2, 3)),
            dma((2,)),
            pltpu.SemaphoreType.REGULAR,
            pltpu.SemaphoreType.REGULAR,
            pltpu.SemaphoreType.REGULAR((3,)),
            pltpu.SemaphoreType.REGULAR,
        ],
        compiler_params=pltpu.CompilerParams(vmem_limit_bytes=VMEM_LIMIT, collective_id=number, has_side_effects=True),
        cost_estimate=pl.CostEstimate(
            flops=(12 if saved is not None else 16) * t * d * f, bytes_accessed=30 * t * f, transcendentals=t * f
        ),
        name=f"backward_{number}",
    )(a, h, dy, wg, wu, wd, *(saved or ()))
    return out[:4]


def solution(mesh):
    def step(x, dy, *weights):
        def fetched(number):
            return [lax.all_gather(w[number], "s", axis=0, tiled=True) for w in weights]

        x, dy = x[0], dy[0]
        wg, wu, wd = fetched(0)
        a0, hid, g, u = gate_up(x, wg, wu)
        h, a1 = down(hid, wd, x)
        by_h, *top = backward(a1, h, dy, *fetched(1), None, 1)
        by_x, *bottom = backward(a0, x, by_h, wg, wu, wd, (g, u), 0)
        return (by_x[None], *(jnp.stack(pair) for pair in zip(bottom, top, strict=True)))

    states, cut = P(("rep", "r", "s"), None, None), P(None, "s", None)
    return jax.shard_map(
        step,
        mesh=mesh,
        in_specs=(states, states) + (cut,) * 3,
        out_specs=(states,) + (P("rep", "s", None),) * 3,
        check_vma=False,
    )
```

time: 1090 us -> 832 us (0.76)
  matrix products: 740 us -> 0 us
  Pallas kernels: 0 us -> 610 us
  waiting for transfers between devices: 243 us -> 176 us
  local copies, waits for them, and re-layouts: 49.3 us -> 18.6 us
  other arithmetic: 37.1 us -> 7.2 us
    dot_general x17 -> x0, matrix products: 740 us -> none  [the longest x6 271 us: layer(): up = jnp.dot(a, w['w_up'], preferred_element_type=jnp.float32)]
    pallas_call x0 -> x4, Pallas kernels: none -> 610 us  [the longest x2 503 us: backward(): pl.pallas_call(functools.partial(backward_kernel, saved is not None), in_...]
    all_gather x6, waiting for transfers between devices: 43.9 us -> 174 us  [fetched(): return [lax.all_gather(w[number], 's', axis=0, tiled=True) for w in weights]]
    psum x1 -> x0, waiting for transfers between devices: 124 us -> none  [summed(): lax.psum(lax.psum_scatter(term, 's', scatter_dimension=0, tiled=True), 'r')]
    reduce_scatter x6 -> x0, waiting for transfers between devices: 72.9 us -> none  [summed(): lax.psum_scatter(term, 's', scatter_dimension=0, tiled=True)]
    unnamed x33 -> x11, local copies, waits for them, and re-layouts: 39.3 us -> 8.73 us
    broadcast_in_dim x1 -> x0, other arithmetic: 12.1 us -> none  [step(): by_h[None]]
    add_any x1 -> x0, other arithmetic: 10.9 us -> none  [normed(): wide = h.astype(jnp.float32)]
  transfers between devices with their start and end apart: 13 -> 6, of which waited for: 7 -> 4; matrix products, arithmetic and copies ran while one was open for 57% -> 1% of each run, Pallas kernels for 0% -> 13%
where the time goes in v1:
time: 832 us; the launch traced here: 826 us
  Pallas kernels  610 us (73%)
  waiting for transfers between devices  176 us (21%)
  local copies, waits for them, and re-layouts  18.6 us (2%)
  between operations  14.6 us (2%)
    pallas_call x2, Pallas kernels, backward(): pl.pallas_call(functools.partial(backward_kernel, saved is not None), in_...  503 us
    all_gather x6, waiting for transfers between devices, fetched(): return [lax.all_gather(w[number], 's', axis=0, tiled=True) for w in weights]  174 us
    pallas_call x1, Pallas kernels, gate_up(): pl.pallas_call(gate_up_kernel, grid=(t // tm,), in_specs=[part(d), whole,...  67.9 us
    pallas_call x1, Pallas kernels, down(): pl.pallas_call(down_kernel, grid=(t // tm,), in_specs=[part(f), pl.BlockS...  38.7 us
  transfers between devices with their start and end apart: 6, of which 4 were waited for; matrix products, arithmetic and copies ran while one was open for 1% of the time, Pallas kernels for 13%

profile of v1, /device:TPU:0, one launch (start us, length us, event | category | flops | bytes accessed | tf_op | source)
XLA Modules:
  0.0 826.1 jit_solution(9130563087296292001)
XLA Ops:
  7.2 0.0 copy-start
  7.2 0.0 all-gather.13.cloned.1.call-start
  7.2 4.0 fusion.2
  11.2 0.0 all-gather.13.cloned.1.call-update
  11.2 0.0 all-gather.15.cloned.1.call-start
  11.3 0.0 copy-done
  11.3 1.9 fusion.1
  13.2 0.0 all-gather.15.cloned.1.call-update
  13.3 0.0 all-gather.17.cloned.1.call-start
  13.3 3.9 fusion
  17.3 0.0 all-gather.17.cloned.1.call-update
  17.3 0.0 all-gather.19.cloned.1.call-start
  17.3 0.5 all-gather.19.cloned.1.call-update
  17.9 0.0 all-gather.21.cloned.1.call-start
  17.9 0.5 all-gather.21.cloned.1.call-update
  18.4 0.0 all-gather.23.cloned.1.call-start
  18.5 0.5 all-gather.23.cloned.1.call-update
  19.0 41.2 %all-gather.13.cloned.1.call-done = bf16[1,1024,3200]{2,1,0:T(8,128)(2,1)} async-done(((bf16[1,256,3200]{2,1,0:T(8,128)(2,1)}), bf16[1,1024,3200]{2,1,0:T(8,128)(2,1)}) %all-gather.13.cloned.1.call-update) | async-done | bytes 6553616 | tf_op jit(solution)/shard_map/all_gather | solution.py:583
  60.3 48.2 %all-gather.15.cloned.1.call-done = bf16[1,1024,3200]{2,1,0:T(8,128)(2,1)} async-done(((bf16[1,256,3200]{2,1,0:T(8,128)(2,1)}), bf16[1,1024,3200]{2,1,0:T(8,128)(2,1)}) %all-gather.15.cloned.1.call-update) | async-done | bytes 6553616 | tf_op jit(solution)/shard_map/all_gather | solution.py:583
  108.4 67.9 %gate_up.1 = (bf16[4096,1024]{1,0:T(8,128)(2,1)}, bf16[4096,3200]{1,0:T(8,128)(2,1)}, f32[4096,3200]{1,0:T(8,128)}, f32[4096,3200]{1,0:T(8,128)}) custom-call(bf16[4096,1024]{1,0:T(8,128)(2,1)} %bitcast.23, bf16[1024,3200]{1,0:T(8,128)(2,1)} %bitcast.26, bf16[1024,3200]{1,0:T(8,128)(2,1)} %bitcast.28), custom_call_target="tpu_custom_call" | custom-call | flops 53687091200 | bytes 157286400 | tf_op jit(solution)/shard_map/gate_up/pallas_call | solution.py:55
  176.3 38.7 %down.1 = (bf16[4096,1024]{1,0:T(8,128)(2,1)}, bf16[4096,1024]{1,0:T(8,128)(2,1)}) custom-call(bf16[4096,3200]{1,0:T(8,128)(2,1)} %get-tuple-element.19.hid_ref, bf16[3200,1024]{1,0:T(8,128)(2,1)} %bitcast.30, bf16[4096,1024]{1,0:T(8,128)(2,1)} %bitcast.24), custom_call_target="tpu_custom_call" | custom-call | flops 26843545600 | bytes 26214400 | tf_op jit(solution)/shard_map/down/pallas_call | solution.py:79
  215.0 37.1 %all-gather.21.cloned.1.call-done = bf16[1,1024,3200]{2,1,0:T(8,128)(2,1)} async-done(((bf16[1,256,3200]{2,1,0:T(8,128)(2,1)}), bf16[1,1024,3200]{2,1,0:T(8,128)(2,1)}) %all-gather.21.cloned.1.call-update) | async-done | bytes 6553616 | tf_op jit(solution)/shard_map/all_gather | solution.py:583
  252.1 47.5 %all-gather.23.cloned.1.call-done = bf16[1,3200,1024]{2,1,0:T(8,128)(2,1)} async-done(((bf16[1,800,1024]{2,1,0:T(8,128)(2,1)}), bf16[1,3200,1024]{2,1,0:T(8,128)(2,1)}) %all-gather.23.cloned.1.call-update) | async-done | bytes 6553616 | tf_op jit(solution)/shard_map/all_gather | solution.py:583
  299.6 268.1 %backward_1.1 = (bf16[4096,1024]{1,0:T(8,128)(2,1)}, bf16[256,3200]{1,0:T(8,128)(2,1)}, bf16[256,3200]{1,0:T(8,128)(2,1)}, bf16[800,1024]{1,0:T(8,128)(2,1)}, bf...) custom-call(bf16[4096,1024]{1,0:T(8,128)(2,1)} %get-tuple-element.20.refs_0_, ...), custom_call_target="tpu_custom_call" | custom-call | flops 214748364800 | bytes 393216000 | tf_op jit(solution)/shard_map/backward_1/pallas_call | solution.py:547
  567.7 235.2 %backward_0.1 = (bf16[4096,1024]{1,0:T(8,128)(2,1)}, bf16[256,3200]{1,0:T(8,128)(2,1)}, bf16[256,3200]{1,0:T(8,128)(2,1)}, bf16[800,1024]{1,0:T(8,128)(2,1)}, bf...) custom-call(bf16[4096,1024]{1,0:T(8,128)(2,1)} %get-tuple-element.18.refs_0_, bf16[4096,1024]{1,0:T(8,128)(2,1)} %bitcast.25, ...), custom_call_target="tpu_custom_call" | custom-call | flops 161061273600 | bytes 393216000 | tf_op jit(solution)/shard_map/backward_0/pallas_call | solution.py:547
  802.9 0.0 copy-start.1
  802.9 0.0 copy-start.2
  802.9 4.1 pad_maximum_fusion.2
  807.0 0.0 copy-done.3
  807.0 1.0 copy-done.4
  808.0 3.1 pad_maximum_fusion
  811.1 7.8 copy.10
  (6 shorter events, 0.0 us)
Async XLA Ops:
  7.2 4.1 copy-start
  7.2 53.1 %all-gather.13.cloned.1.call-start = ((), (), s32[]{:S(2)}) async-start(), calls=%async_computation | async-start | bytes 8192000 | tf_op jit(solution)/shard_map/all_gather | solution.py:583
  11.2 97.2 %all-gather.15.cloned.1.call-start = ((), (), s32[]{:S(2)}) async-start(), calls=%async_computation.1 | async-start | bytes 8192000 | tf_op jit(solution)/shard_map/all_gather | solution.py:583
  13.3 163.1 %all-gather.17.cloned.1.call-start = ((), (), s32[]{:S(2)}) async-start(), calls=%async_computation.2 | async-start | bytes 8192000 | tf_op jit(solution)/shard_map/all_gather | solution.py:583
  17.3 197.7 %all-gather.19.cloned.1.call-start = ((), (), s32[]{:S(2)}) async-start(), calls=%async_computation.3 | async-start | bytes 8192000 | tf_op jit(solution)/shard_map/all_gather | solution.py:583
  17.9 234.3 %all-gather.21.cloned.1.call-start = ((), (), s32[]{:S(2)}) async-start(), calls=%async_computation.4 | async-start | bytes 8192000 | tf_op jit(solution)/shard_map/all_gather | solution.py:583
  18.4 281.1 %all-gather.23.cloned.1.call-start = ((), (), s32[]{:S(2)}) async-start(), calls=%async_computation.5 | async-start | bytes 8192000 | tf_op jit(solution)/shard_map/all_gather | solution.py:583
  802.9 4.1 copy-start.1
  802.9 4.1 copy-start.2
  802.9 4.1 copy-start.3
  802.9 5.1 copy-start.4
Sparse Core Ops, SparseCore 0:
  11.4 48.8 all-gather.12
  62.4 46.0 all-gather.14
  110.0 46.0 all-gather.16
  158.0 46.0 all-gather.18
  206.1 46.0 all-gather.20
  253.5 46.0 all-gather.22

commit v2 on v1

--- a/solution.py
+++ b/solution.py
@@ -33,61 +33,6 @@
     return pl.ds(pl.multiple_of(start, unit) if size % unit == 0 else start, size)
 
 
-def gate_up_kernel(x_ref, wg_ref, wu_ref, a_ref, hid_ref, g_ref, u_ref):
-    wide = x_ref[...].astype(F32)
-    a = (wide * scale_of(wide)).astype(BF)
-    a_ref[...] = a
-    width = wg_ref.shape[1] // CHUNKS
-    for j in range(CHUNKS):
-        c = pl.ds(j * width, width)
-        both = dot(a, jnp.concatenate([wg_ref[:, c], wu_ref[:, c]], 1))
-        g, u = both[:, :width], both[:, width:]
-        g_ref[:, c], u_ref[:, c] = g, u
-        hid_ref[:, c] = (g * jax.nn.sigmoid(g) * u).astype(BF)
-
-
-def gate_up(x, wg, wu):
-    t, d = x.shape
-    f = wg.shape[1]
-    tm = t // 16
-    whole = pl.BlockSpec((d, f), lambda i: (0, 0), pipeline_mode=pl.Buffered(1))
-    part = lambda n: pl.BlockSpec((tm, n), lambda i: (i, 0))
-    return pl.pallas_call(
-        gate_up_kernel,
-        grid=(t // tm,),
-        in_specs=[part(d), whole, whole],
-        out_specs=[part(d), part(f), part(f), part(f)],
-        out_shape=[jax.ShapeDtypeStruct((t, n), k) for n, k in ((d, BF), (f, BF), (f, F32), (f, F32))],
-        compiler_params=pltpu.CompilerParams(vmem_limit_bytes=VMEM_LIMIT, dimension_semantics=("arbitrary",)),
-        cost_estimate=pl.CostEstimate(flops=4 * t * d * f, bytes_accessed=12 * t * f, transcendentals=t * f),
-        name="gate_up",
-    )(x, wg, wu)
-
-
-def down_kernel(hid_ref, w_ref, x_ref, h_ref, a_ref):
-    h = (x_ref[...].astype(F32) + dot(hid_ref[...], w_ref[...]).astype(BF).astype(F32)).astype(BF)
-    h_ref[...] = h
-    wide = h.astype(F32)
-    a_ref[...] = (wide * scale_of(wide)).astype(BF)
-
-
-def down(hid, w, x):
-    t, d = x.shape
-    f = w.shape[0]
-    tm = t // 8
-    part = lambda n: pl.BlockSpec((tm, n), lambda i: (i, 0))
-    return pl.pallas_call(
-        down_kernel,
-        grid=(t // tm,),
-        in_specs=[part(f), pl.BlockSpec((f, d), lambda i: (0, 0), pipeline_mode=pl.Buffered(1)), part(d)],
-        out_specs=[part(d), part(d)],
-        out_shape=[jax.ShapeDtypeStruct((t, d), BF)] * 2,
-        compiler_params=pltpu.CompilerParams(vmem_limit_bytes=VMEM_LIMIT, dimension_semantics=("arbitrary",)),
-        cost_estimate=pl.CostEstimate(flops=2 * t * d * f, bytes_accessed=2 * t * f, transcendentals=0),
-        name="down",
-    )(hid, w, x)
-
-
 def here():
     s = lax.axis_index("s")
     return lax.axis_index("r"), lax.div(s, 2), lax.rem(s, 2)
@@ -109,7 +54,395 @@
         copy.wait()
 
 
-def backward_kernel(saved, *refs):
+def guarded(condition, do):
+    @pl.when(condition)
+    def _():
+        do()
+
+
+def neighbours():
+    me_r, x, core = here()
+    partner = {"s": x * 2 + (1 - core)}
+    across = {"s": (1 - x) * 2 + core}
+    peers = [(lax.rem(me_r + k, 4), {"r": lax.rem(me_r + k, 4)}) for k in (1, 2, 3)]
+    return partner, across, peers
+
+
+def meet(everyone):
+    barrier = pltpu.get_barrier_semaphore()
+    for p in everyone:
+        pl.semaphore_signal(barrier, inc=1, device_id=p, device_id_type=MESH)
+    pl.semaphore_wait(barrier, len(everyone))
+
+
+def forward_kernel(x_hbm, wg_own, wu_own, wd_own, *refs):
+    a_hbm, hid_hbm, g_hbm, u_hbm, h_hbm, a1_hbm, wg_all, wu_all, wd_all = refs[:9]
+    (a_v, w_v, x_v, hid_v, g_v, u_v, wd_v, hi_v, xi_v, ho_v, ao_v, bg_v, bd_v) = refs[9:22]
+    sem_x, sem_y, sem_d, sem_b, sem_w, sem_i, sem_ao, sem_o, sem_wd, sem_p, sem_q = refs[22:]
+    t, d = x_hbm.shape
+    f = hid_hbm.shape[1]
+    c = f // CHUNKS
+    me_r, x, core = here()
+    me, oa = 2 * x + core, 2 * (1 - x) + core
+    partner, across, peers = neighbours()
+    meet([partner, across] + [p for _, p in peers])
+
+    p0 = pieces(c)[0][1]
+    runs = [(0, p0), (p0, c - p0)] + [(c * k, c) for k in range(1, CHUNKS)]
+
+    class Piece:
+        def __init__(self, number, layer, own, full, lo, width):
+            self.n = number
+            held = own.shape[1]
+            unit = 16 if held % 16 == 0 and held >= 128 else 4
+            self.q = held * 3 // 16 // unit * unit
+            self.direct = held - 4 * self.q
+            self.held = held
+            self.own = lambda at, size: own.at[layer, rows(at, size), pl.ds(lo, width)]
+            self.full = lambda at, size: full.at[layer, rows(at, size), pl.ds(lo, width)]
+
+        def quarter(self):
+            at, to = self.direct + me_r * self.q, me * self.held
+            return send(self.own(at, self.q), self.full(to + at, self.q), (sem_x.at[0, self.n, 0], sem_x.at[1, self.n, 0]), across)
+
+        def straight(self):
+            sems = (sem_x.at[0, self.n, 1], sem_x.at[1, self.n, 1])
+            return send(self.own(0, self.direct), self.full(me * self.held, self.direct), sems, across)
+
+        def y_copies(self):
+            block = self.full(oa * self.held + self.direct + me_r * self.q, self.q)
+            return [send(block, block, (sem_y.at[0, self.n, k], sem_y.at[1, self.n, k]), to) for k, (_, to) in enumerate(peers)]
+
+        def mine(self):
+            sems = (sem_d.at[0, self.n, 0], sem_d.at[1, self.n, 0])
+            return send(self.own(0, self.held), self.full(me * self.held, self.held), sems, partner)
+
+        def theirs(self):
+            block = self.full(oa * self.held, self.held)
+            return send(block, block, (sem_d.at[0, self.n, 1], sem_d.at[1, self.n, 1]), partner)
+
+    gate_up = [
+        [Piece(2 * p + m, 0, own, full, lo, width) for m, (own, full) in enumerate(((wg_own, wg_all), (wu_own, wu_all)))]
+        for p, (lo, width) in enumerate(runs)
+    ]
+    n = 2 * len(runs)
+    d0, g1, u1, d1 = (
+        [Piece(n, 0, wd_own, wd_all, 0, d)],
+        [Piece(n + 1, 1, wg_own, wg_all, 0, f)],
+        [Piece(n + 2, 1, wu_own, wu_all, 0, f)],
+        [Piece(n + 3, 1, wd_own, wd_all, 0, d)],
+    )
+
+    def h0(group):
+        for p in group:
+            p.quarter().start()
+            p.straight().start()
+        for p in group:
+            p.mine().start()
+
+    def h1(group):
+        for p in group:
+            p.quarter().wait()
+            start(p.y_copies())
+
+    def h2(group):
+        for p in group:
+            p.straight().wait()
+            wait(p.y_copies())
+            p.theirs().start()
+
+    def h3(group):
+        for p in group:
+            p.mine().wait()
+            p.theirs().wait()
+
+    blocks = [(wg_own, wg_all, bg_v), (wu_own, wu_all, bg_v), (wd_own, wd_all, bd_v)]
+
+    def b_in(layer, m):
+        own, _, via = blocks[m]
+        return pltpu.make_async_copy(own.at[layer], via, sem_b.at[m // 2, 0])
+
+    def b_out(layer, m):
+        own, full, via = blocks[m]
+        return pltpu.make_async_copy(via, full.at[layer, rows(me * own.shape[1], own.shape[1]), :], sem_b.at[m // 2, 1])
+
+    def b0(layer, m):
+        b_in(layer, m).start()
+
+    def b1(layer, m):
+        b_in(layer, m).wait()
+        b_out(layer, m).start()
+
+    def b2(layer, m):
+        b_out(layer, m).wait()
+
+    def load(k):
+        lo, width = runs[k]
+        at = pl.ds(lo, width)
+        return [
+            pltpu.make_async_copy(full.at[0, :, at], w_v.at[k % 2, :, pl.ds(m * c, width)], sem_w.at[k % 2, m])
+            for m, full in enumerate((wg_all, wu_all))
+        ]
+
+    def load_d():
+        return [pltpu.make_async_copy(wd_all.at[0], wd_v, sem_wd)]
+
+    h0(gate_up[0])
+    h0(gate_up[1])
+    b0(0, 0)
+    b0(0, 2)
+
+    tm = t // 4
+
+    def x_copy(i):
+        return [pltpu.make_async_copy(x_hbm.at[rows(i * tm, tm), :], x_v.at[i % 2], sem_i.at[i % 2])]
+
+    def a_copy(i):
+        return [pltpu.make_async_copy(a_v.at[rows(i * tm, tm), :], a_hbm.at[rows(i * tm, tm), :], sem_ao.at[i])]
+
+    start(x_copy(0))
+    h0(gate_up[2])
+    for i in range(4):
+        if i < 3:
+            start(x_copy(i + 1))
+        wait(x_copy(i))
+
+        def norm(k, _, i=i):
+            at = rows(k * (tm // 4), tm // 4)
+            wide = x_v[i % 2, at, :].astype(F32)
+            a_v[rows(i * tm + k * (tm // 4), tm // 4), :] = (wide * scale_of(wide)).astype(BF)
+            return 0
+
+        lax.fori_loop(0, 4, norm, 0)
+        start(a_copy(i))
+        if i == 0:
+            b1(0, 0)
+            b1(0, 2)
+        if i == 1:
+            b2(0, 0)
+            b0(0, 1)
+            h1(gate_up[0])
+        if i == 2:
+            b1(0, 1)
+            h0(gate_up[3])
+    h1(gate_up[1])
+    h2(gate_up[0])
+    b2(0, 1)
+    h3(gate_up[0])
+    start(load(0))
+
+    def o_copies(slot, i, lo, width):
+        at = (rows(i * tm, tm), rows(lo, width, 128))
+        near = pl.ds(0, width)
+        return [
+            pltpu.make_async_copy(v.at[slot, :, near], o.at[at], sem_o.at[slot, m])
+            for m, (v, o) in enumerate(((hid_v, hid_hbm), (g_v, g_hbm), (u_v, u_hbm)))
+        ]
+
+    def compute(i, lo, width, parts, w_slot):
+        slot = lax.rem(i, 2)
+        a = a_v[rows(i * tm, tm), :]
+        for at, w in parts:
+            both = dot(a, jnp.concatenate([w_v[w_slot, :, pl.ds(at, w)], w_v[w_slot, :, pl.ds(c + at, w)]], 1))
+            g, u = both[:, :w], both[:, w:]
+            g_v[slot, :, pl.ds(at, w)] = g
+            u_v[slot, :, pl.ds(at, w)] = u
+            hid_v[slot, :, pl.ds(at, w)] = (g * jax.nn.sigmoid(g) * u).astype(BF)
+        start(o_copies(slot, i, lo, width))
+
+    td = t // 8
+
+    def i_copies(m):
+        at = rows(m * td, td)
+        return [
+            pltpu.make_async_copy(hid_hbm.at[at, :], hi_v.at[lax.rem(m, 2)], sem_p.at[lax.rem(m, 2), 0]),
+            pltpu.make_async_copy(x_hbm.at[at, :], xi_v.at[lax.rem(m, 2)], sem_p.at[lax.rem(m, 2), 1]),
+        ]
+
+    def q_copies(m):
+        at = rows(m * td, td)
+        return [
+            pltpu.make_async_copy(ho_v.at[lax.rem(m, 2)], h_hbm.at[at, :], sem_q.at[lax.rem(m, 2), 0]),
+            pltpu.make_async_copy(ao_v.at[lax.rem(m, 2)], a1_hbm.at[at, :], sem_q.at[lax.rem(m, 2), 1]),
+        ]
+
+    gu = gate_up
+    before = {
+        (0, 1): lambda: (b0(1, 0), b2(0, 2), b0(1, 2)),
+        (0, 2): lambda: (h2(gu[1]), h1(gu[2])),
+        (0, 3): lambda: (h3(gu[1]), start(load(1)), h0(gu[4])),
+        (1, 1): lambda: (b1(1, 0), b1(1, 2)),
+        (1, 2): lambda: h1(gu[3]),
+        (1, 3): lambda: (h2(gu[2]), b2(1, 0), b0(1, 1), b2(1, 2)),
+        (2, -1): lambda: (h3(gu[2]), start(load(2)), h0(gu[5])),
+        (2, 0): lambda: (h1(gu[4]), b1(1, 1)),
+        (2, 1): lambda: (h2(gu[3]), h0(d0)),
+        (2, 2): lambda: (h1(gu[5]), h3(gu[3]), start(load(3))),
+        (2, 3): lambda: (h2(gu[4]), h0(g1), b2(1, 1)),
+        (3, 1): lambda: (h2(gu[5]), h3(gu[4])),
+        (3, 3): lambda: (h1(d0), h3(gu[5]), h0(u1)),
+        (4, -1): lambda: start(load(4)),
+        (4, 1): lambda: h0(d1),
+        (5, -1): lambda: start(load(5)),
+        (5, 0): lambda: h1(g1),
+        (5, 1): lambda: h2(d0),
+        (5, 3): lambda: (h3(d0), start(load_d()), start(i_copies(0))),
+    }
+    def at_point(k, i):
+        for (k0, i0), do in before.items():
+            if isinstance(k, int):
+                if k0 == k and i0 >= 0:
+                    guarded(i == i0, do)
+            elif k0 > 1 and (i0 < 0) == (i is None):
+                guarded(k == k0 if i is None else jnp.logical_and(k == k0, i == i0), do)
+
+    for k in (0, 1):
+        lo, width = runs[k]
+        first = max(width // 2 // 128 * 128, width // 2 if width < 256 else 0)
+        wait(load(k))
+
+        def tile(i, _, k=k, lo=lo, width=width, first=first):
+            at_point(k, i)
+            slot = lax.rem(i, 2)
+
+            @pl.when(i >= 2)
+            def _():
+                wait(o_copies(slot, i - 2, lo, width))
+
+            if k == 1:
+
+                @pl.when(i < 2)
+                def _():
+                    wait(o_copies(slot, i + 2, *runs[0]))
+
+            compute(i, lo, width, ((0, first), (first, width - first)), k)
+            return 0
+
+        lax.fori_loop(0, 4, tile, 0)
+
+    def run(k, _):
+        lo = (k - 1) * c
+        w_slot = lax.rem(k, 2)
+        at_point(k, None)
+        for k0 in range(2, len(runs)):
+
+            @pl.when(k == k0)
+            def _(k0=k0):
+                wait(load(k0))
+
+        def tile(i, _):
+            at_point(k, i)
+            slot = lax.rem(i, 2)
+
+            @pl.when(i >= 2)
+            def _():
+                wait(o_copies(slot, i - 2, lo, c))
+
+            @pl.when(jnp.logical_and(i < 2, k == 2))
+            def _():
+                wait(o_copies(slot, i + 2, *runs[1]))
+
+            @pl.when(jnp.logical_and(i < 2, k > 2))
+            def _():
+                wait(o_copies(slot, i + 2, lo - c, c))
+
+            compute(i, lo, c, pieces(c), w_slot)
+            return 0
+
+        lax.fori_loop(0, 4, tile, 0)
+        return 0
+
+    lax.fori_loop(2, len(runs), run, 0)
+    last = len(runs) - 1
+    wait(o_copies(0, 2, *runs[last]))
+    wait(o_copies(1, 3, *runs[last]))
+    wait(load_d())
+    before = {
+        0: lambda: h1(u1),
+        1: lambda: h2(g1),
+        3: lambda: h3(g1),
+        4: lambda: h1(d1),
+        5: lambda: h2(u1),
+        7: lambda: h3(u1),
+    }
+
+    def tile(m, _):
+        slot = lax.rem(m, 2)
+
+        @pl.when(m < 7)
+        def _():
+            start(i_copies(m + 1))
+
+        for m0, do in before.items():
+            guarded(m == m0, do)
+        wait(i_copies(m))
+
+        @pl.when(m > 1)
+        def _():
+            wait(q_copies(m - 2))
+
+        h = (xi_v[slot].astype(F32) + dot(hi_v[slot], wd_v[...]).astype(BF).astype(F32)).astype(BF)
+        ho_v[slot] = h
+        wide = h.astype(F32)
+        ao_v[slot] = (wide * scale_of(wide)).astype(BF)
+        start(q_copies(m))
+        return 0
+
+    lax.fori_loop(0, 8, tile, 0)
+    h2(d1)
+    wait(q_copies(6))
+    wait(q_copies(7))
+    for i in range(4):
+        wait(a_copy(i))
+    h3(d1)
+
+
+def forward(x, wg, wu, wd):
+    t, d = x.shape
+    f = wg.shape[2]
+    c = f // CHUNKS
+    n, dma = 2 * CHUNKS + 6, pltpu.SemaphoreType.DMA
+    shapes = [((t, d), BF), ((t, f), BF), ((t, f), F32), ((t, f), F32), ((t, d), BF), ((t, d), BF)]
+    shapes += [((2, d, f), BF), ((2, d, f), BF), ((2, f, d), BF)]
+    return pl.pallas_call(
+        forward_kernel,
+        in_specs=[ANY] * 4,
+        out_specs=[ANY] * len(shapes),
+        out_shape=[jax.ShapeDtypeStruct(*s) for s in shapes],
+        scratch_shapes=[
+            pltpu.VMEM((t, d), BF),
+            pltpu.VMEM((2, d, 2 * c), BF),
+            pltpu.VMEM((2, t // 4, d), BF),
+            pltpu.VMEM((2, t // 4, c), BF),
+            pltpu.VMEM((2, t // 4, c), F32),
+            pltpu.VMEM((2, t // 4, c), F32),
+            pltpu.VMEM((f, d), BF),
+            pltpu.VMEM((2, t // 8, f), BF),
+            pltpu.VMEM((2, t // 8, d), BF),
+            pltpu.VMEM((2, t // 8, d), BF),
+            pltpu.VMEM((2, t // 8, d), BF),
+            pltpu.VMEM(wg.shape[1:], BF),
+            pltpu.VMEM(wd.shape[1:], BF),
+            dma((2, n, 2)),
+            dma((2, n, 3)),
+            dma((2, n, 2)),
+            dma((2, 2)),
+            dma((2, 2)),
+            dma((2,)),
+            dma((4,)),
+            dma((2, 3)),
+            dma,
+            dma((2, 2)),
+            dma((2, 2)),
+        ],
+        compiler_params=pltpu.CompilerParams(vmem_limit_bytes=VMEM_LIMIT, collective_id=2, has_side_effects=True),
+        cost_estimate=pl.CostEstimate(flops=6 * t * d * f, bytes_accessed=16 * t * f, transcendentals=t * f),
+        name="forward",
+    )(x, wg, wu, wd)
+
+
+def backward_kernel(layer, *refs):
+    saved = layer == 0
     n_in = 8 if saved else 6
     a_hbm, h_hbm, dy_hbm, wg_hbm, wu_hbm, wd_hbm = refs[:6]
     g_hbm, u_hbm = refs[6:n_in] if saved else (None, None)
@@ -117,7 +450,7 @@
     (stg, buf_d, acc, buf_x, s_x, s_r, buf_r, s_g, sem_d, sem_x, sem_r, sem_g, sem_gl, free_d, free_x, free_r, entered) = refs[n_in + 6 :]
 
     t, d = a_hbm.shape
-    f = wd_hbm.shape[0]
+    f = wd_hbm.shape[1]
     c = f // CHUNKS
     own = d // 4
     quarter = own // 4
@@ -125,15 +458,9 @@
     rd = own_d // 5
     qd = d // 4
     me_r, x, core = here()
-    partner = {"s": x * 2 + (1 - core)}
-    across = {"s": (1 - x) * 2 + core}
-    peers = [(lax.rem(me_r + k, 4), {"r": lax.rem(me_r + k, 4)}) for k in (1, 2, 3)]
+    partner, across, peers = neighbours()
     everyone = [partner, across] + [p for _, p in peers]
-
-    barrier = pltpu.get_barrier_semaphore()
-    for p in everyone:
-        pl.semaphore_signal(barrier, inc=1, device_id=p, device_id_type=MESH)
-    pl.semaphore_wait(barrier, 5)
+    meet(everyone)
 
     def d_copies():
         return [
@@ -220,10 +547,10 @@
         def w_copies(j):
             slot = lax.rem(j, 2)
             at = rows(j * c, c, 128)
-            w = [pltpu.make_async_copy(wd_hbm.at[at, :], wd_v.at[slot], sem_w.at[slot, 0])]
+            w = [pltpu.make_async_copy(wd_hbm.at[layer, at, :], wd_v.at[slot], sem_w.at[slot, 0])]
             if not saved:
-                w.append(pltpu.make_async_copy(wg_hbm.at[:, at], wgu_v.at[slot, :, pl.ds(0, c)], sem_w.at[slot, 1]))
-                w.append(pltpu.make_async_copy(wu_hbm.at[:, at], wgu_v.at[slot, :, pl.ds(c, c)], sem_w.at[slot, 2]))
+                w.append(pltpu.make_async_copy(wg_hbm.at[layer, :, at], wgu_v.at[slot, :, pl.ds(0, c)], sem_w.at[slot, 1]))
+                w.append(pltpu.make_async_copy(wu_hbm.at[layer, :, at], wgu_v.at[slot, :, pl.ds(c, c)], sem_w.at[slot, 2]))
             return w
 
         def s_copies(n):
@@ -374,7 +701,7 @@
             return [pltpu.make_async_copy(o_v.at[slot], out_hbm.at[rows(i * ta, ta), :], sem_o.at[slot])]
 
         def w_copy(k):
-            return [pltpu.make_async_copy((wg_hbm, wu_hbm)[k], (wg_v, wu_v)[k], sem_w.at[k])]
+            return [pltpu.make_async_copy((wg_hbm, wu_hbm)[k].at[layer], (wg_v, wu_v)[k], sem_w.at[k])]
 
         def dd_copies(k):
             far = [
@@ -538,14 +865,14 @@
     )
 
 
-def backward(a, h, dy, wg, wu, wd, saved, number):
+def backward(a, h, dy, wg, wu, wd, saved, layer):
     t, d = a.shape
-    f = wd.shape[0]
+    f = wd.shape[1]
     c = f // CHUNKS
     own, dma = d // 4, pltpu.SemaphoreType.DMA
     shapes = [(t, d), (own, f), (own, f), (f // 4, d), (t, 2 * f), (f, d)]
     out = pl.pallas_call(
-        functools.partial(backward_kernel, saved is not None),
+        functools.partial(backward_kernel, layer),
         in_specs=[ANY] * (8 if saved is not None else 6),
         out_specs=[ANY] * len(shapes),
         out_shape=[jax.ShapeDtypeStruct(s, BF) for s in shapes],
@@ -568,26 +895,21 @@
             pltpu.SemaphoreType.REGULAR((3,)),
             pltpu.SemaphoreType.REGULAR,
         ],
-        compiler_params=pltpu.CompilerParams(vmem_limit_bytes=VMEM_LIMIT, collective_id=number, has_side_effects=True),
+        compiler_params=pltpu.CompilerParams(vmem_limit_bytes=VMEM_LIMIT, collective_id=layer, has_side_effects=True),
         cost_estimate=pl.CostEstimate(
             flops=(12 if saved is not None else 16) * t * d * f, bytes_accessed=30 * t * f, transcendentals=t * f
         ),
-        name=f"backward_{number}",
+        name=f"backward_{layer}",
     )(a, h, dy, wg, wu, wd, *(saved or ()))
     return out[:4]
 
 
 def solution(mesh):
     def step(x, dy, *weights):
-        def fetched(number):
-            return [lax.all_gather(w[number], "s", axis=0, tiled=True) for w in weights]
-
         x, dy = x[0], dy[0]
-        wg, wu, wd = fetched(0)
-        a0, hid, g, u = gate_up(x, wg, wu)
-        h, a1 = down(hid, wd, x)
-        by_h, *top = backward(a1, h, dy, *fetched(1), None, 1)
-        by_x, *bottom = backward(a0, x, by_h, wg, wu, wd, (g, u), 0)
+        a0, _, g, u, h, a1, *whole = forward(x, *weights)
+        by_h, *top = backward(a1, h, dy, *whole, None, 1)
+        by_x, *bottom = backward(a0, x, by_h, *whole, (g, u), 0)
         return (by_x[None], *(jnp.stack(pair) for pair in zip(bottom, top, strict=True)))
 
     states, cut = P(("rep", "r", "s"), None, None), P(None, "s", None)

time: 832 us -> 663 us (0.80)
  waiting for transfers between devices: 176 us -> 0 us
  Pallas kernels: 610 us -> 640 us
  between operations: 14.6 us -> 1.12 us
  local copies, waits for them, and re-layouts: 18.6 us -> 7.76 us
    all_gather x6 -> x0, waiting for transfers between devices: 174 us -> none  [fetched(): return [lax.all_gather(w[number], 's', axis=0, tiled=True) for w in weights]]
    pallas_call x4 -> x3, Pallas kernels: 610 us -> 640 us  [the longest x2 503 us: backward(): pl.pallas_call(functools.partial(backward_kernel, layer), in_specs=[ANY]...]
    slice x3 -> x0, local copies, waits for them, and re-layouts: 9.87 us -> none  [fetched(): return [lax.all_gather(w[number], 's', axis=0, tiled=True) for w in weights]]
  transfers between devices with their start and end apart: 6 -> 0, of which waited for: 4 -> 0; matrix products, arithmetic and copies ran while one was open for 1% -> 0% of each run, Pallas kernels for 13% -> 0%
where the time goes in v2:
time: 663 us; the launch traced here: 656 us
  Pallas kernels  640 us (97%)
  local copies, waits for them, and re-layouts  7.76 us (1%)
  other arithmetic  7.15 us (1%)
    pallas_call x2, Pallas kernels, backward(): pl.pallas_call(functools.partial(backward_kernel, layer), in_specs=[ANY]...  503 us
    pallas_call x1, Pallas kernels, forward(): pl.pallas_call(forward_kernel, in_specs=[ANY] * 4, out_specs=[ANY] * len(...  137 us

profile of v2, /device:TPU:0, one launch (start us, length us, event | category | flops | bytes accessed | tf_op | source)
XLA Modules:
  0.0 655.8 jit_solution(350908078621981040)
XLA Ops:
  0.6 136.9 %forward.1 = (bf16[4096,1024]{1,0:T(8,128)(2,1)}, bf16[4096,3200]{1,0:T(8,128)(2,1)}, f32[4096,3200]{1,0:T(8,128)}, f32[4096,3200]{1,0:T(8,128)}, bf16[4096,1024...) custom-call(bf16[4096,1024]{1,0:T(8,128)(2,1)} %bitcast.17, ...), custom_call_target="tpu_custom_call" | custom-call | flops 80530636800 | bytes 209715200 | tf_op jit(solution)/shard_map/forward/pallas_call | solution.py:407
  137.5 266.9 %backward_1.1 = (bf16[4096,1024]{1,0:T(8,128)(2,1)}, bf16[256,3200]{1,0:T(8,128)(2,1)}, bf16[256,3200]{1,0:T(8,128)(2,1)}, bf16[800,1024]{1,0:T(8,128)(2,1)}, bf...) custom-call(bf16[4096,1024]{1,0:T(8,128)(2,1)} %get-tuple-element.21.refs_0_, ...), custom_call_target="tpu_custom_call" | custom-call | flops 214748364800 | bytes 393216000 | tf_op jit(solution)/shard_map/backward_1/pallas_call | solution.py:874
  404.4 236.0 %backward_0.1 = (bf16[4096,1024]{1,0:T(8,128)(2,1)}, bf16[256,3200]{1,0:T(8,128)(2,1)}, bf16[256,3200]{1,0:T(8,128)(2,1)}, bf16[800,1024]{1,0:T(8,128)(2,1)}, bf...) custom-call(bf16[4096,1024]{1,0:T(8,128)(2,1)} %get-tuple-element.20.refs_0_, bf16[4096,1024]{1,0:T(8,128)(2,1)} %bitcast.18, ...), custom_call_target="tpu_custom_call" | custom-call | flops 161061273600 | bytes 393216000 | tf_op jit(solution)/shard_map/backward_0/pallas_call | solution.py:874
  640.4 0.0 copy-start
  640.4 0.0 copy-start.1
  640.4 5.2 pad_maximum_fusion
  645.6 0.0 copy-done
  645.6 0.0 copy-done.1
  645.6 2.0 pad_maximum_fusion.2
  647.6 7.8 %copy.10 = bf16[1,4096,1024]{2,1,0:T(8,128)(2,1)} copy(bf16[1,4096,1024]{2,1,0:T(8,128)(2,1)} %bitcast.9) | data formatting | bytes 16777216
Async XLA Ops:
  640.4 5.2 copy-start
  640.4 5.2 copy-start.1

commit v3 on v2

--- a/solution.py
+++ b/solution.py
@@ -189,47 +189,51 @@
 
     h0(gate_up[0])
     h0(gate_up[1])
+
+    tm = t // 4
+    td = t // 8
+    tn = min(64, td)
+
+    def x_copy(i):
+        return [pltpu.make_async_copy(x_hbm.at[rows(i * td, td), :], x_v.at[i % 4], sem_i.at[i % 4])]
+
+    def a_copy(i):
+        return [pltpu.make_async_copy(a_v.at[rows(i * td, td), :], a_hbm.at[rows(i * td, td), :], sem_ao.at[i])]
+
+    for i in range(4):
+        start(x_copy(i))
     b0(0, 0)
     b0(0, 2)
-
-    tm = t // 4
-
-    def x_copy(i):
-        return [pltpu.make_async_copy(x_hbm.at[rows(i * tm, tm), :], x_v.at[i % 2], sem_i.at[i % 2])]
-
-    def a_copy(i):
-        return [pltpu.make_async_copy(a_v.at[rows(i * tm, tm), :], a_hbm.at[rows(i * tm, tm), :], sem_ao.at[i])]
-
-    start(x_copy(0))
     h0(gate_up[2])
-    for i in range(4):
-        if i < 3:
-            start(x_copy(i + 1))
+    for i in range(8):
         wait(x_copy(i))
 
         def norm(k, _, i=i):
-            at = rows(k * (tm // 4), tm // 4)
-            wide = x_v[i % 2, at, :].astype(F32)
-            a_v[rows(i * tm + k * (tm // 4), tm // 4), :] = (wide * scale_of(wide)).astype(BF)
+            wide = x_v[i % 4, rows(k * tn, tn), :].astype(F32)
+            a_v[rows(i * td + k * tn, tn), :] = (wide * scale_of(wide)).astype(BF)
             return 0
 
-        lax.fori_loop(0, 4, norm, 0)
+        lax.fori_loop(0, td // tn, norm, 0)
         start(a_copy(i))
-        if i == 0:
+        if i < 4:
+            start(x_copy(i + 4))
+        if i == 1:
             b1(0, 0)
             b1(0, 2)
-        if i == 1:
+        if i == 2:
+            h1(gate_up[0])
             b2(0, 0)
             b0(0, 1)
-            h1(gate_up[0])
-        if i == 2:
+        if i == 4:
             b1(0, 1)
+            h1(gate_up[1])
+        if i == 5:
+            h2(gate_up[0])
+            b2(0, 1)
             h0(gate_up[3])
-    h1(gate_up[1])
-    h2(gate_up[0])
-    b2(0, 1)
     h3(gate_up[0])
     start(load(0))
+    h0(gate_up[4])
 
     def o_copies(slot, i, lo, width):
         at = (rows(i * tm, tm), rows(lo, width, 128))
@@ -245,12 +249,12 @@
         for at, w in parts:
             both = dot(a, jnp.concatenate([w_v[w_slot, :, pl.ds(at, w)], w_v[w_slot, :, pl.ds(c + at, w)]], 1))
             g, u = both[:, :w], both[:, w:]
-            g_v[slot, :, pl.ds(at, w)] = g
-            u_v[slot, :, pl.ds(at, w)] = u
-            hid_v[slot, :, pl.ds(at, w)] = (g * jax.nn.sigmoid(g) * u).astype(BF)
+            s = jax.nn.sigmoid(g)
+            silu = g * s
+            g_v[slot, :, pl.ds(at, w)] = u * (s + silu * (1.0 - s))
+            u_v[slot, :, pl.ds(at, w)] = silu
+            hid_v[slot, :, pl.ds(at, w)] = (silu * u).astype(BF)
         start(o_copies(slot, i, lo, width))
-
-    td = t // 8
 
     def i_copies(m):
         at = rows(m * td, td)
@@ -259,35 +263,35 @@
             pltpu.make_async_copy(x_hbm.at[at, :], xi_v.at[lax.rem(m, 2)], sem_p.at[lax.rem(m, 2), 1]),
         ]
 
-    def q_copies(m):
-        at = rows(m * td, td)
-        return [
-            pltpu.make_async_copy(ho_v.at[lax.rem(m, 2)], h_hbm.at[at, :], sem_q.at[lax.rem(m, 2), 0]),
-            pltpu.make_async_copy(ao_v.at[lax.rem(m, 2)], a1_hbm.at[at, :], sem_q.at[lax.rem(m, 2), 1]),
-        ]
+    def h_copy(m):
+        return [pltpu.make_async_copy(ho_v.at[lax.rem(m, 2)], h_hbm.at[rows(m * td, td), :], sem_q.at[lax.rem(m, 2), 0])]
+
+    def a1_copy(m):
+        return [pltpu.make_async_copy(ao_v.at[lax.rem(m, 2)], a1_hbm.at[rows(m * td, td), :], sem_q.at[lax.rem(m, 2), 1])]
 
     gu = gate_up
     before = {
         (0, 1): lambda: (b0(1, 0), b2(0, 2), b0(1, 2)),
         (0, 2): lambda: (h2(gu[1]), h1(gu[2])),
-        (0, 3): lambda: (h3(gu[1]), start(load(1)), h0(gu[4])),
-        (1, 1): lambda: (b1(1, 0), b1(1, 2)),
-        (1, 2): lambda: h1(gu[3]),
-        (1, 3): lambda: (h2(gu[2]), b2(1, 0), b0(1, 1), b2(1, 2)),
-        (2, -1): lambda: (h3(gu[2]), start(load(2)), h0(gu[5])),
-        (2, 0): lambda: (h1(gu[4]), b1(1, 1)),
-        (2, 1): lambda: (h2(gu[3]), h0(d0)),
-        (2, 2): lambda: (h1(gu[5]), h3(gu[3]), start(load(3))),
-        (2, 3): lambda: (h2(gu[4]), h0(g1), b2(1, 1)),
-        (3, 1): lambda: (h2(gu[5]), h3(gu[4])),
-        (3, 3): lambda: (h1(d0), h3(gu[5]), h0(u1)),
-        (4, -1): lambda: start(load(4)),
-        (4, 1): lambda: h0(d1),
-        (5, -1): lambda: start(load(5)),
-        (5, 0): lambda: h1(g1),
-        (5, 1): lambda: h2(d0),
-        (5, 3): lambda: (h3(d0), start(load_d()), start(i_copies(0))),
+        (0, 3): lambda: (h3(gu[1]), start(load(1)), h0(gu[5])),
+        (1, 0): lambda: (b1(1, 0), b1(1, 2)),
+        (1, 1): lambda: (h2(gu[2]), h1(gu[3]), h0(d0)),
+        (1, 2): lambda: (h3(gu[2]), start(load(2))),
+        (1, 3): lambda: (b2(1, 0), b0(1, 1), b2(1, 2)),
+        (2, 0): lambda: (h2(gu[3]), h1(gu[4]), b1(1, 1), h0(g1)),
+        (2, 1): lambda: (h3(gu[3]), start(load(3))),
+        (2, 2): lambda: h1(gu[5]),
+        (2, 3): lambda: (h2(gu[4]), b2(1, 1)),
+        (3, 0): lambda: (h3(gu[4]), start(load(4)), h0(u1)),
+        (3, 1): lambda: (h2(gu[5]), h1(d0)),
+        (3, 2): lambda: h3(gu[5]),
+        (4, 0): lambda: (start(load(5)), h0(d1)),
+        (4, 2): lambda: (h2(d0), h1(g1)),
+        (5, 0): lambda: (h3(d0), start(load_d())),
+        (5, 2): lambda: (h2(g1), h1(u1)),
+        (5, 3): lambda: start(i_copies(0)),
     }
+
     def at_point(k, i):
         for (k0, i0), do in before.items():
             if isinstance(k, int):
@@ -354,20 +358,25 @@
 
     lax.fori_loop(2, len(runs), run, 0)
     last = len(runs) - 1
-    wait(o_copies(0, 2, *runs[last]))
-    wait(o_copies(1, 3, *runs[last]))
     wait(load_d())
     before = {
-        0: lambda: h1(u1),
-        1: lambda: h2(g1),
-        3: lambda: h3(g1),
-        4: lambda: h1(d1),
-        5: lambda: h2(u1),
-        7: lambda: h3(u1),
+        0: lambda: h3(g1),
+        3: lambda: h2(u1),
+        4: lambda: h3(u1),
+        5: lambda: h1(d1),
     }
+
+    def norm_of(m):
+        wide = ho_v[lax.rem(m, 2)].astype(F32)
+        ao_v[lax.rem(m, 2)] = (wide * scale_of(wide)).astype(BF)
 
     def tile(m, _):
         slot = lax.rem(m, 2)
+
+        @pl.when(m == 3)
+        def _():
+            wait(o_copies(0, 2, *runs[last]))
+            wait(o_copies(1, 3, *runs[last]))
 
         @pl.when(m < 7)
         def _():
@@ -379,21 +388,33 @@
 
         @pl.when(m > 1)
         def _():
-            wait(q_copies(m - 2))
-
-        h = (xi_v[slot].astype(F32) + dot(hi_v[slot], wd_v[...]).astype(BF).astype(F32)).astype(BF)
-        ho_v[slot] = h
-        wide = h.astype(F32)
-        ao_v[slot] = (wide * scale_of(wide)).astype(BF)
-        start(q_copies(m))
+            wait(h_copy(m - 2))
+
+        @pl.when(m > 2)
+        def _():
+            wait(a1_copy(m - 3))
+
+        norm_of(m + 1)
+        ho_v[slot] = (xi_v[slot].astype(F32) + dot(hi_v[slot], wd_v[...]).astype(BF).astype(F32)).astype(BF)
+        start(h_copy(m))
+
+        @pl.when(m > 0)
+        def _():
+            start(a1_copy(m - 1))
+
         return 0
 
     lax.fori_loop(0, 8, tile, 0)
+    wait(a1_copy(5))
+    norm_of(7)
+    start(a1_copy(7))
+    wait(h_copy(6))
+    wait(h_copy(7))
+    wait(a1_copy(6))
+    wait(a1_copy(7))
+    for i in range(8):
+        wait(a_copy(i))
     h2(d1)
-    wait(q_copies(6))
-    wait(q_copies(7))
-    for i in range(4):
-        wait(a_copy(i))
     h3(d1)
 
 
@@ -412,7 +433,7 @@
         scratch_shapes=[
             pltpu.VMEM((t, d), BF),
             pltpu.VMEM((2, d, 2 * c), BF),
-            pltpu.VMEM((2, t // 4, d), BF),
+            pltpu.VMEM((4, t // 8, d), BF),
             pltpu.VMEM((2, t // 4, c), BF),
             pltpu.VMEM((2, t // 4, c), F32),
             pltpu.VMEM((2, t // 4, c), F32),
@@ -428,8 +449,8 @@
             dma((2, n, 2)),
             dma((2, 2)),
             dma((2, 2)),
-            dma((2,)),
             dma((4,)),
+            dma((8,)),
             dma((2, 3)),
             dma,
             dma((2, 2)),
@@ -443,9 +464,9 @@
 
 def backward_kernel(layer, *refs):
     saved = layer == 0
-    n_in = 8 if saved else 6
+    n_in = 9 if saved else 6
     a_hbm, h_hbm, dy_hbm, wg_hbm, wu_hbm, wd_hbm = refs[:6]
-    g_hbm, u_hbm = refs[6:n_in] if saved else (None, None)
+    g_hbm, u_hbm, hid_hbm = refs[6:n_in] if saved else (None, None, None)
     out_hbm, og_hbm, ou_hbm, od_hbm, dgu_hbm, dwd_hbm = refs[n_in : n_in + 6]
     (stg, buf_d, acc, buf_x, s_x, s_r, buf_r, s_g, sem_d, sem_x, sem_r, sem_g, sem_gl, free_d, free_x, free_r, entered) = refs[n_in + 6 :]
 
@@ -528,12 +549,12 @@
     def e4(p):
         wait(g_copies(p))
 
-    tm = t // 8 if saved else t // 4
+    tm = t // 4
     tiles = t // tm
 
     def chunks(*bufs):
         if saved:
-            a_v, dy_v, wd_v, hid_v, dgs, dst, g_v, u_v, sem_a, sem_w, sem_o, sem_s = bufs
+            a_v, dy_v, wd_v, hid_v, dgs, dst, g_v, u_v, sem_a, sem_w, sem_o, sem_s, sem_h = bufs
         else:
             a_v, dy_v, wd_v, hid_v, dgs, dst, wgu_v, sem_a, sem_w, sem_o = bufs
 
@@ -567,14 +588,19 @@
                 pltpu.make_async_copy(dgs.at[:, pl.ds(c, c)], dgu_hbm.at[:, rows(f + j * c, c, 128)], sem_o.at[1]),
             ]
 
+        def hid_copy(j):
+            return [pltpu.make_async_copy(hid_hbm.at[:, rows(j * c, c, 128)], hid_v, sem_h)]
+
         def dw_copy(j):
             return [pltpu.make_async_copy(dst, dwd_hbm.at[rows(j * c, c), :], sem_o.at[2])]
 
         start(w_copies(0))
-        if saved:
-            start(s_copies(0))
         for i in range(tiles):
             start(a_copies(i))
+            if saved and i == 0:
+                start(s_copies(0))
+        if saved:
+            start(hid_copy(0))
 
         def chunk(j, _):
             slot = lax.rem(j, 2)
@@ -633,19 +659,20 @@
 
                 r = rows(i * tm, tm)
                 for p0, w in pieces(c):
-                    if saved:
-                        g = g_v[lax.rem(n, 2), :, pl.ds(p0, w)]
-                        u = u_v[lax.rem(n, 2), :, pl.ds(p0, w)]
-                    else:
+                    if not saved:
                         a = a_v[r, :]
                         both = dot(a, jnp.concatenate([wgu_v[slot, :, pl.ds(p0, w)], wgu_v[slot, :, pl.ds(c + p0, w)]], 1))
                         g, u = both[:, :w], both[:, w:]
                     dh = dot(dy_v[r, :], wd_v[slot, pl.ds(p0, w), :], NT).astype(BF).astype(F32)
-                    s = jax.nn.sigmoid(g)
-                    silu = g * s
-                    hid_v[r, pl.ds(p0, w)] = (silu * u).astype(BF)
-                    dgs[r, pl.ds(c + p0, w)] = (dh * silu).astype(BF)
-                    dgs[r, pl.ds(p0, w)] = (dh * u * (s + silu * (1.0 - s))).astype(BF)
+                    if saved:
+                        by_gate, by_up = g_v[lax.rem(n, 2), :, pl.ds(p0, w)], u_v[lax.rem(n, 2), :, pl.ds(p0, w)]
+                    else:
+                        s = jax.nn.sigmoid(g)
+                        by_up = g * s
+                        by_gate = u * (s + by_up * (1.0 - s))
+                        hid_v[r, pl.ds(p0, w)] = (by_up * u).astype(BF)
+                    dgs[r, pl.ds(c + p0, w)] = (dh * by_up).astype(BF)
+                    dgs[r, pl.ds(p0, w)] = (dh * by_gate).astype(BF)
                 return 0
 
             lax.fori_loop(0, tiles, tile, 0)
@@ -655,9 +682,16 @@
             def _():
                 wait(dw_copy(j - 1))
 
+            if saved:
+                wait(hid_copy(j))
             for p0, w in pieces(c):
                 dst[pl.ds(p0, w), :] = dot(hid_v[:, pl.ds(p0, w)], dy_v[...], TN).astype(BF)
             start(dw_copy(j))
+            if saved:
+
+                @pl.when(j + 1 < CHUNKS)
+                def _():
+                    start(hid_copy(j + 1))
 
             @pl.when(j >= 2)
             def _():
@@ -681,19 +715,26 @@
     ]
     bufs += [pltpu.VMEM((2, tm, c), F32)] * 2 if saved else [pltpu.VMEM((2, d, 2 * c), BF)]
     bufs += [pltpu.SemaphoreType.DMA((2, tiles)), pltpu.SemaphoreType.DMA((2, 3)), pltpu.SemaphoreType.DMA((3,))]
-    bufs += [pltpu.SemaphoreType.DMA((2, 2))] if saved else []
+    bufs += [pltpu.SemaphoreType.DMA((2, 2)), pltpu.SemaphoreType.DMA] if saved else []
     pl.run_scoped(chunks, *bufs)
 
     ta = t // 8
 
-    def last(wg_v, wu_v, dgu_v, h_v, dy_v, o_v, own_v, bd_v, ac_v, bx_v, sx_v, br_v, sg_v, sem_w, sem_i, sem_o, dd, dx, dr, dg, dl):
+    def last(wg_v, wu_v, dgu_v, h_v, dy_v, o_v, bg_v, bu_v, own_v, bd_v, ac_v, bx_v, sx_v, br_v, sg_v, sem_w, sem_i, sem_o, dd, dx, dr, dg, dl):
+        def i_copy(i, m):
+            slot = lax.rem(i, 2)
+            part = pl.ds(m * f, f)
+            return pltpu.make_async_copy(dgu_hbm.at[rows(i * ta, ta), part], dgu_v.at[slot, :, part], sem_i.at[slot, m])
+
         def i_copies(i):
+            return [i_copy(i, 0), i_copy(i, 1)]
+
+        def h_copies(i):
             slot = lax.rem(i, 2)
             at = rows(i * ta, ta)
             return [
-                pltpu.make_async_copy(dgu_hbm.at[at, :], dgu_v.at[slot], sem_i.at[slot, 0]),
-                pltpu.make_async_copy(h_hbm.at[at, :], h_v.at[slot], sem_i.at[slot, 1]),
-                pltpu.make_async_copy(dy_hbm.at[at, :], dy_v.at[slot], sem_i.at[slot, 2]),
+                pltpu.make_async_copy(h_hbm.at[at, :], h_v.at[slot], sem_i.at[slot, 2]),
+                pltpu.make_async_copy(dy_hbm.at[at, :], dy_v.at[slot], sem_i.at[slot, 3]),
             ]
 
         def o_copy(i):
@@ -762,20 +803,18 @@
 
         end = CHUNKS - 1
         todo = {
-            0: [lambda: e4(end - 2), lambda: e2(end - 1, False, False), lambda: e0(end, False)],
-            1: [lambda: e1(end, False, True)],
-            2: [lambda: f1(0), lambda: f1(1)],
-            3: [lambda: e3(end - 1, False), lambda: f1(2)],
-            4: [lambda: f1(3), lambda: f1(4)],
-            5: [lambda: e2(end, False, True)],
-            6: [lambda: e4(end - 1)],
+            1: [lambda: f1(0), lambda: f1(1)],
+            2: [lambda: e3(end - 1, False), lambda: f1(2)],
+            3: [lambda: f1(3), lambda: f1(4)],
+            5: [lambda: e2(end, False, True), lambda: e4(end - 1)],
             7: [lambda: f2(0)],
-            8: [lambda: e3(end, True)],
-            9: [lambda: f2(1), lambda: f3(0)],
-            11: [lambda: f2(2), lambda: f3(1)],
-            12: [lambda: e4(end)],
-            13: [lambda: f2(3), lambda: f3(2)],
-            15: [lambda: f2(4), lambda: f3(3)],
+            8: [lambda: e3(end, True), lambda: f2(1)],
+            10: [lambda: f2(2), lambda: f3(0)],
+            11: [lambda: e4(end), lambda: f3(1)],
+            12: [lambda: f2(3)],
+            13: [lambda: f3(2)],
+            14: [lambda: f2(4)],
+            15: [lambda: f3(3)],
         }
 
         def events(i, half):
@@ -787,55 +826,73 @@
                         for do in does:
                             do()
 
-        start(w_copy(0))
-        start(i_copies(0))
-        start(w_copy(1))
-        for p in everyone:
-            pl.semaphore_signal(entered, inc=1, device_id=p, device_id_type=MESH)
-        pl.semaphore_wait(entered, 5)
-        for k in range(5):
-            f0(k)
-
-        def tile(i, _):
+        def tail(i):
             slot = lax.rem(i, 2)
-
-            @pl.when(i + 1 < 8)
-            def _():
-                start(i_copies(i + 1))
-
-            events(i, 0)
-            wait(i_copies(i))
-
-            @pl.when(i == 0)
-            def _():
-                wait(w_copy(0))
-
-            by_g = dot(dgu_v[slot, :, pl.ds(0, f)], wg_v[...], NT).astype(BF)
-            o_v[slot] = by_g
-            events(i, 1)
-
-            @pl.when(i == 0)
-            def _():
-                wait(w_copy(1))
-
-            by_u = dot(dgu_v[slot, :, pl.ds(f, f)], wu_v[...], NT).astype(BF)
-            by_a = (o_v[slot].astype(F32) + by_u.astype(F32)).astype(BF).astype(F32)
+            by_a = (bg_v[...].astype(F32) + bu_v[...].astype(F32)).astype(BF).astype(F32)
             wide = h_v[slot].astype(F32)
             scale = scale_of(wide)
             by_scale = jnp.sum(by_a * wide, -1, keepdims=True)
             by_wide = (by_a * scale - (by_scale * scale * scale * scale * (1.0 / d)) * wide).astype(BF)
             o_v[slot] = (dy_v[slot].astype(F32) + by_wide.astype(F32)).astype(BF)
-            start(o_copy(i))
-
-            @pl.when(i >= 1)
-            def _():
-                wait(o_copy(i - 1))
-
+
+        def by_g(i):
+            bg_v[...] = dot(dgu_v[lax.rem(i, 2), :, pl.ds(0, f)], wg_v[...], NT).astype(BF)
+
+        def by_u(i):
+            bu_v[...] = dot(dgu_v[lax.rem(i, 2), :, pl.ds(f, f)], wu_v[...], NT).astype(BF)
+
+        start(w_copy(0))
+        i_copy(0, 0).start()
+        start(w_copy(1))
+        i_copy(0, 1).start()
+        start(h_copies(0))
+        for p in everyone:
+            pl.semaphore_signal(entered, inc=1, device_id=p, device_id_type=MESH)
+        e4(end - 2)
+        e2(end - 1, False, False)
+        e0(end, False)
+        wait(w_copy(0))
+        i_copy(0, 0).wait()
+        pl.semaphore_wait(entered, 5)
+        for k in range(5):
+            f0(k)
+        e1(end, False, True)
+        start(i_copies(1))
+        by_g(0)
+        events(0, 1)
+        wait(w_copy(1))
+        i_copy(0, 1).wait()
+        by_u(0)
+
+        def tile(i, _):
+            @pl.when(i + 1 < 8)
+            def _():
+                start(i_copies(i + 1))
+
+            events(i, 0)
+            wait(i_copies(i))
+            wait(h_copies(i - 1))
+
+            @pl.when(i >= 3)
+            def _():
+                wait(o_copy(i - 3))
+
+            tail(i - 1)
+            by_g(i)
+            start(o_copy(i - 1))
+            start(h_copies(i))
+            events(i, 1)
+            by_u(i)
             return 0
 
-        lax.fori_loop(0, 8, tile, 0)
+        lax.fori_loop(1, 8, tile, 0)
+        f3(4)
+        wait(h_copies(7))
+        wait(o_copy(5))
+        tail(7)
+        start(o_copy(7))
+        wait(o_copy(6))
         wait(o_copy(7))
-        f3(4)
         for k in range(5):
             f4(k)
 
@@ -847,6 +904,8 @@
         pltpu.VMEM((2, ta, d), BF),
         pltpu.VMEM((2, ta, d), BF),
         pltpu.VMEM((2, ta, d), BF),
+        pltpu.VMEM((ta, d), BF),
+        pltpu.VMEM((ta, d), BF),
         pltpu.VMEM((5, 2, rd, d), BF),
         pltpu.VMEM((5, 2, rd, d), BF),
         pltpu.VMEM((5, rd, d), F32),
@@ -855,7 +914,7 @@
         pltpu.VMEM((5, 3, rd, qd), BF),
         pltpu.VMEM((5, rd, qd), BF),
         pltpu.SemaphoreType.DMA((2,)),
-        pltpu.SemaphoreType.DMA((2, 3)),
+        pltpu.SemaphoreType.DMA((2, 4)),
         pltpu.SemaphoreType.DMA((2,)),
         pltpu.SemaphoreType.DMA((2, 5, 2)),
         pltpu.SemaphoreType.DMA((2, 5)),
@@ -873,7 +932,7 @@
     shapes = [(t, d), (own, f), (own, f), (f // 4, d), (t, 2 * f), (f, d)]
     out = pl.pallas_call(
         functools.partial(backward_kernel, layer),
-        in_specs=[ANY] * (8 if saved is not None else 6),
+        in_specs=[ANY] * (9 if saved is not None else 6),
         out_specs=[ANY] * len(shapes),
         out_shape=[jax.ShapeDtypeStruct(s, BF) for s in shapes],
         scratch_shapes=[
@@ -904,13 +963,55 @@
     return out[:4]
 
 
+def placed_kernel(*refs):
+    ins, outs = refs[:7], refs[7:11]
+    bufs, sem_in, sem_out = refs[11:18], refs[18], refs[19]
+    parts = 8
+    copies = []
+    for n, (src, buf) in enumerate(zip(ins, bufs, strict=True)):
+        dst = outs[0] if n == 0 else outs[(n + 1) // 2].at[(n - 1) % 2]
+        step = src.shape[0] // (parts if n == 0 else 1)
+        for p in range(parts if n == 0 else 1):
+            at = pl.ds(p * step, step)
+            k = len(copies)
+            copies.append(
+                (
+                    pltpu.make_async_copy(src.at[at, :], buf.at[at, :], sem_in.at[k]),
+                    pltpu.make_async_copy(buf.at[at, :], dst.at[at, :], sem_out.at[k]),
+                )
+            )
+    for first, _ in copies:
+        first.start()
+    for first, second in copies:
+        first.wait()
+        second.start()
+    for _, second in copies:
+        second.wait()
+
+
+def placed(by_x, *sums):
+    ins = (by_x, *sums)
+    outs = [by_x.shape] + [(2, *s.shape) for s in sums[::2]]
+    return pl.pallas_call(
+        placed_kernel,
+        in_specs=[ANY] * len(ins),
+        out_specs=[ANY] * len(outs),
+        out_shape=[jax.ShapeDtypeStruct(s, BF) for s in outs],
+        scratch_shapes=[pltpu.VMEM(a.shape, BF) for a in ins]
+        + [pltpu.SemaphoreType.DMA((14,)), pltpu.SemaphoreType.DMA((14,))],
+        compiler_params=pltpu.CompilerParams(vmem_limit_bytes=VMEM_LIMIT),
+        name="placed",
+    )(*ins)
+
+
 def solution(mesh):
     def step(x, dy, *weights):
         x, dy = x[0], dy[0]
-        a0, _, g, u, h, a1, *whole = forward(x, *weights)
+        a0, hid, g, u, h, a1, *whole = forward(x, *weights)
         by_h, *top = backward(a1, h, dy, *whole, None, 1)
-        by_x, *bottom = backward(a0, x, by_h, *whole, (g, u), 0)
-        return (by_x[None], *(jnp.stack(pair) for pair in zip(bottom, top, strict=True)))
+        by_x, *bottom = backward(a0, x, by_h, *whole, (g, u, hid), 0)
+        by_x, *sums = placed(by_x, *(part for pair in zip(bottom, top, strict=True) for part in pair))
+        return (by_x[None], *sums)
 
     states, cut = P(("rep", "r", "s"), None, None), P(None, "s", None)
     return jax.shard_map(

time: 663 us -> 632 us (0.953)
  Pallas kernels: 640 us -> 624 us
  local copies, waits for them, and re-layouts: 7.76 us -> 0 us
  other arithmetic: 7.15 us -> 0 us
    pallas_call x2, Pallas kernels: 503 us -> 482 us  [backward(): pl.pallas_call(functools.partial(backward_kernel, layer), in_specs=[ANY]...]
    pallas_call x0 -> x1, Pallas kernels: none -> 13.1 us  [placed(): pl.pallas_call(placed_kernel, in_specs=[ANY] * len(ins), out_specs=[ANY]...]
    unnamed x5 -> x0, local copies, waits for them, and re-layouts: 7.76 us -> none
    pallas_call x1, Pallas kernels: 137 us -> 129 us  [forward(): pl.pallas_call(forward_kernel, in_specs=[ANY] * 4, out_specs=[ANY] * len(...]
    another operation x2 -> x0, other arithmetic: 7.15 us -> none  [step(): jnp.stack(pair)]
where the time goes in v3:
time: 632 us; the launch traced here: 625 us
  Pallas kernels  624 us (99%)
    pallas_call x2, Pallas kernels, backward(): pl.pallas_call(functools.partial(backward_kernel, layer), in_specs=[ANY]...  482 us
    pallas_call x1, Pallas kernels, forward(): pl.pallas_call(forward_kernel, in_specs=[ANY] * 4, out_specs=[ANY] * len(...  129 us
    pallas_call x1, Pallas kernels, placed(): pl.pallas_call(placed_kernel, in_specs=[ANY] * len(ins), out_specs=[ANY]...  13.1 us

profile of v3, /device:TPU:0, one launch (start us, length us, event | category | flops | bytes accessed | tf_op | source)
XLA Modules:
  0.0 624.8 jit_solution(5336715731886122837)
XLA Ops:
  0.6 129.1 %forward.1 = (bf16[4096,1024]{1,0:T(8,128)(2,1)}, bf16[4096,3200]{1,0:T(8,128)(2,1)}, f32[4096,3200]{1,0:T(8,128)}, f32[4096,3200]{1,0:T(8,128)}, bf16[4096,1024...) custom-call(bf16[4096,1024]{1,0:T(8,128)(2,1)} %bitcast.4, ...), custom_call_target="tpu_custom_call" | custom-call | flops 80530636800 | bytes 209715200 | tf_op jit(solution)/shard_map/forward/pallas_call | solution.py:428
  129.8 263.0 %backward_1.1 = (bf16[4096,1024]{1,0:T(8,128)(2,1)}, bf16[256,3200]{1,0:T(8,128)(2,1)}, bf16[256,3200]{1,0:T(8,128)(2,1)}, bf16[800,1024]{1,0:T(8,128)(2,1)}, bf...) custom-call(bf16[4096,1024]{1,0:T(8,128)(2,1)} %get-tuple-element.26.refs_0_, ...), custom_call_target="tpu_custom_call" | custom-call | flops 214748364800 | bytes 393216000 | tf_op jit(solution)/shard_map/backward_1/pallas_call | solution.py:933
  392.8 218.7 %backward_0.1 = (bf16[4096,1024]{1,0:T(8,128)(2,1)}, bf16[256,3200]{1,0:T(8,128)(2,1)}, bf16[256,3200]{1,0:T(8,128)(2,1)}, bf16[800,1024]{1,0:T(8,128)(2,1)}, bf...) custom-call(bf16[4096,1024]{1,0:T(8,128)(2,1)} %get-tuple-element.25.refs_0_, bf16[4096,1024]{1,0:T(8,128)(2,1)} %bitcast.5, ...), custom_call_target="tpu_custom_call" | custom-call | flops 161061273600 | bytes 393216000 | tf_op jit(solution)/shard_map/backward_0/pallas_call | solution.py:933
  611.5 13.1 %placed.1 = (bf16[4096,1024]{1,0:T(8,128)(2,1)}, bf16[2,256,3200]{2,1,0:T(8,128)(2,1)}, bf16[2,256,3200]{2,1,0:T(8,128)(2,1)}, bf16[2,800,1024]{2,1,0:T(8,128)(2,1)}) custom-call(bf16[4096,1024]{1,0:T(8,128)(2,1)} %get-tuple-element.35.refs_0_, bf16[256,3200]{1,0:T(8,128)(2,1)} %get-tuple-element.36.refs_1_, bf16[256,3200]{1,0:T(8,128)(2,1)} %get-tuple-element.37.refs_2_, ...), custom_call_target="tpu_custom_call" | custom-call | tf_op jit(solution)/shard_map/placed/pallas_call | solution.py:995

commit v4 on v3

--- a/solution.py
+++ b/solution.py
@@ -85,16 +85,14 @@
     me_r, x, core = here()
     me, oa = 2 * x + core, 2 * (1 - x) + core
     partner, across, peers = neighbours()
-    meet([partner, across] + [p for _, p in peers])
-
-    p0 = pieces(c)[0][1]
+    p0 = 256 if c > 512 else c // 2
     runs = [(0, p0), (p0, c - p0)] + [(c * k, c) for k in range(1, CHUNKS)]
 
     class Piece:
         def __init__(self, number, layer, own, full, lo, width):
             self.n = number
             held = own.shape[1]
-            unit = 16 if held % 16 == 0 and held >= 128 else 4
+            unit = 16 if held >= 128 else 4
             self.q = held * 3 // 16 // unit * unit
             self.direct = held - 4 * self.q
             self.held = held
@@ -187,9 +185,6 @@
     def load_d():
         return [pltpu.make_async_copy(wd_all.at[0], wd_v, sem_wd)]
 
-    h0(gate_up[0])
-    h0(gate_up[1])
-
     tm = t // 4
     td = t // 8
     tn = min(64, td)
@@ -204,6 +199,9 @@
         start(x_copy(i))
     b0(0, 0)
     b0(0, 2)
+    meet([partner, across] + [p for _, p in peers])
+    h0(gate_up[0])
+    h0(gate_up[1])
     h0(gate_up[2])
     for i in range(8):
         wait(x_copy(i))
@@ -462,13 +460,44 @@
     )(x, wg, wu, wd)
 
 
+PARTS = 5
+LATE = 2
+TILES = 8
+LEFT = 2
+
+
+def input_gradient(f, dgu, wg, wu, h, dy, bg_v, bu_v):
+    d = bg_v.shape[-1]
+
+    def by_gate():
+        bg_v[...] = dot(dgu[:, pl.ds(0, f)], wg[...], NT).astype(BF)
+
+    def by_up():
+        bu_v[...] = dot(dgu[:, pl.ds(f, f)], wu[...], NT).astype(BF)
+
+    def rest():
+        by_a = (bg_v[...].astype(F32) + bu_v[...].astype(F32)).astype(BF).astype(F32)
+        wide = h[...].astype(F32)
+        scale = scale_of(wide)
+        by_scale = jnp.sum(by_a * wide, -1, keepdims=True)
+        by_wide = (by_a * scale - (by_scale * scale * scale * scale * (1.0 / d)) * wide).astype(BF)
+        return (dy[...].astype(F32) + by_wide.astype(F32)).astype(BF)
+
+    return by_gate, by_up, rest
+
+
 def backward_kernel(layer, *refs):
     saved = layer == 0
-    n_in = 9 if saved else 6
     a_hbm, h_hbm, dy_hbm, wg_hbm, wu_hbm, wd_hbm = refs[:6]
-    g_hbm, u_hbm, hid_hbm = refs[6:n_in] if saved else (None, None, None)
-    out_hbm, og_hbm, ou_hbm, od_hbm, dgu_hbm, dwd_hbm = refs[n_in : n_in + 6]
-    (stg, buf_d, acc, buf_x, s_x, s_r, buf_r, s_g, sem_d, sem_x, sem_r, sem_g, sem_gl, free_d, free_x, free_r, entered) = refs[n_in + 6 :]
+    if saved:
+        g_hbm, u_hbm, hid_hbm, upper_hbm = refs[6:10]
+        out_hbm, og_hbm, ou_hbm, od_hbm, od1_hbm, dgu_hbm, dwd_hbm = refs[10:17]
+        refs = refs[17:]
+    else:
+        out_hbm, og_hbm, ou_hbm, od_hbm, dgu_hbm, dwd_hbm = refs[6:12]
+        refs = refs[12:]
+    (stg, buf_d, acc, buf_x, s_x, s_r, buf_r, s_g, sem_d, sem_x, sem_r, sem_g, sem_gl, free_d, free_x, free_r) = refs[:16]
+    own_v, bd_v, ac_v, bx_v, sx_v, br_v, sg_v, dd, dx, dr, dg, dl, free_dd, free_dx, free_dr = refs[16:]
 
     t, d = a_hbm.shape
     f = wd_hbm.shape[1]
@@ -476,12 +505,10 @@
     own = d // 4
     quarter = own // 4
     own_d = f // 4
-    rd = own_d // 5
+    rd = own_d // PARTS
     qd = d // 4
     me_r, x, core = here()
     partner, across, peers = neighbours()
-    everyone = [partner, across] + [p for _, p in peers]
-    meet(everyone)
 
     def d_copies():
         return [
@@ -549,29 +576,185 @@
     def e4(p):
         wait(g_copies(p))
 
+    late = LATE if saved else 0
+    pieces_d = PARTS + late if saved else PARTS - LATE
+
+    def source(q):
+        return (upper_hbm, PARTS - late + q) if q < late else (dwd_hbm, q - late)
+
+    def dd_far(q):
+        src, part = source(q)
+        n = q % 2
+        return [
+            send(src.at[rows((2 * m + 1 - core) * own_d + part * rd, rd), :], bd_v.at[n, m], (dd.at[0, n, m], dd.at[1, n, m]), partner)
+            for m in range(2)
+        ]
+
+    def dd_near(q):
+        src, part = source(q)
+        n = q % 2
+        return [
+            pltpu.make_async_copy(src.at[rows((2 * m + core) * own_d + part * rd, rd), :], own_v.at[n, m], dl.at[0, n, m])
+            for m in range(2)
+        ]
+
+    def dx_copies(q):
+        n = q % 2
+        return [send(sx_v.at[n], bx_v.at[n], (dx.at[0, n], dx.at[1, n]), across)]
+
+    def dr_copies(q):
+        n = q % 2
+        return [
+            send(sx_v.at[n, :, rows(to_r * qd, qd, 128)], br_v.at[n, m], (dr.at[0, n, m], dr.at[1, n, m]), to)
+            for m, (to_r, to) in enumerate(peers)
+        ]
+
+    def dg_copies(q):
+        n = q % 2
+        dst, part = (od1_hbm, q) if q < late else (od_hbm, q - late)
+        at = (rows(part * rd, rd), rows(me_r * qd, qd, 128))
+        far = [send(sg_v.at[n], dst.at[at], (dg.at[0, n, m], dg.at[1, n, m]), to) for m, (_, to) in enumerate(peers)]
+        return far + [pltpu.make_async_copy(sg_v.at[n], dst.at[at], dl.at[1, n, 0])]
+
+    def f0(q):
+        if q >= 2:
+            pl.semaphore_wait(free_dd, 1)
+        start(dd_far(q))
+        start(dd_near(q))
+
+    def f1(q):
+        n = q % 2
+        wait(dd_near(q))
+        wait(dd_far(q))
+        ac_v[n] = own_v[n, x].astype(F32) + bd_v[n, x].astype(F32)
+        sx_v[n] = (own_v[n, 1 - x].astype(F32) + bd_v[n, 1 - x].astype(F32)).astype(BF)
+        if q + 2 < pieces_d:
+            pl.semaphore_signal(free_dd, inc=1, device_id=partner, device_id_type=MESH)
+        if q >= 2:
+            pl.semaphore_wait(free_dx, 1)
+        start(dx_copies(q))
+
+    def f2(q):
+        n = q % 2
+        wait(dx_copies(q))
+        total = ac_v[n] + bx_v[n].astype(F32)
+        ac_v[n] = total
+        sx_v[n] = total.astype(BF)
+        if q + 2 < pieces_d:
+            pl.semaphore_signal(free_dx, inc=1, device_id=across, device_id_type=MESH)
+        if q >= 2:
+            for m in range(3):
+                pl.semaphore_wait(free_dr.at[m], 1)
+        start(dr_copies(q))
+
+    def f3(q):
+        n = q % 2
+        wait(dr_copies(q))
+        total = ac_v[n, :, rows(me_r * qd, qd, 128)]
+        for m in range(3):
+            total = total + br_v[n, m].astype(F32)
+        sg_v[n] = total.astype(BF)
+        if q + 2 < pieces_d:
+            for m, (_, to) in enumerate(peers):
+                pl.semaphore_signal(free_dr.at[2 - m], inc=1, device_id=to, device_id_type=MESH)
+        start(dg_copies(q))
+
+    def f4(q):
+        wait(dg_copies(q))
+
+    def do(*events):
+        for event in events:
+            event()
+
+    E0 = lambda p: lambda: e0(p, p == 0)
+    E1 = lambda p: lambda: e1(p, p == 0, p == CHUNKS - 1)
+    E2 = lambda p: lambda: e2(p, p == 0, p == CHUNKS - 1)
+    E3 = lambda p: lambda: e3(p, p == CHUNKS - 1)
+    E4 = lambda p: lambda: e4(p)
+    F0, F1, F2, F3, F4 = (lambda q, g=g: lambda: g(q) for g in (f0, f1, f2, f3, f4))
+
     tm = t // 4
     tiles = t // tm
+    if saved:
+        at_start = {0: [F0(0), F0(1)], 1: [F1(0), F1(1)], 3: [F2(0)], 4: [F2(1)]}
+        at_chunk = {
+            (0, 0): [F3(0)],
+            (0, 1): [F3(1), F0(2), F0(3)],
+            (0, 3): [F1(2), F1(3)],
+            (0, 4): [F4(0), F4(1)],
+            (1, 0): [F2(2), E0(0), F0(4)],
+            (1, 2): [F2(3), E1(0)],
+            (1, 4): [F3(2), F1(4)],
+            (2, 0): [F3(3), F4(2), E0(1), F0(5)],
+            (2, 1): [E2(0)],
+            (2, 2): [E1(1)],
+            (2, 4): [F2(4), F1(5)],
+            (3, 0): [F3(4), F4(3), E3(0), E0(2), F0(6)],
+            (3, 1): [E2(1)],
+            (3, 2): [E1(2)],
+            (3, 4): [F4(4), F2(5), F1(6)],
+            (4, 0): [E4(0), E3(1), E0(3)],
+            (4, 2): [F3(5), E2(2), E1(3)],
+        }
+        at_end = {
+            -1: [E0(4), E4(1), E3(2), F2(6)],
+            0: [E2(3), E1(4)],
+            1.5: [F4(5), F3(6), E4(2)],
+            2.5: [E3(3), E2(4)],
+            4: [F4(6), E4(3)],
+            5: [E3(4)],
+        }
+        after = [E4(4)]
+    else:
+        at_start = {}
+        at_chunk = {
+            (1, 0): [E0(0)],
+            (1, 2): [E1(0)],
+            (2, 0): [E2(0), E0(1)],
+            (2, 2): [E1(1)],
+            (2, 4): [E3(0)],
+            (3, 0): [E4(0), E2(1), E0(2)],
+            (3, 2): [E1(2)],
+            (3, 4): [E3(1)],
+            (4, 0): [E4(1), E2(2), E0(3)],
+            (4, 2): [E1(3)],
+            (4, 4): [E3(2)],
+        }
+        at_end = {
+            -1: [E4(2), E2(3), E0(4), F0(0), F0(1)],
+            0: [E1(4)],
+            0.5: [F1(0), F1(1), F0(2)],
+            1: [E3(3)],
+            2: [E2(4)],
+            3: [F2(0), E4(3)],
+            3.5: [E3(4)],
+            4: [F3(0), F2(1), F1(2)],
+            5.5: [F4(0), F2(2)],
+            6: [F3(1), E4(4)],
+            6.5: [F3(2)],
+        }
+        after = [F4(1), F4(2)]
 
     def chunks(*bufs):
         if saved:
-            a_v, dy_v, wd_v, hid_v, dgs, dst, g_v, u_v, sem_a, sem_w, sem_o, sem_s, sem_h = bufs
+            a_v, dy_v, wd_v, dgs, dst, g_v, u_v, sem_a, sem_w, sem_o, sem_s, sem_h = bufs
         else:
             a_v, dy_v, wd_v, hid_v, dgs, dst, wgu_v, sem_a, sem_w, sem_o = bufs
 
-        def a_copies(i):
+        def a_copy(i):
             at = rows(i * tm, tm)
-            return [
-                pltpu.make_async_copy(a_hbm.at[at, :], a_v.at[at, :], sem_a.at[0, i]),
-                pltpu.make_async_copy(dy_hbm.at[at, :], dy_v.at[at, :], sem_a.at[1, i]),
-            ]
+            return [pltpu.make_async_copy(a_hbm.at[at, :], a_v.at[at, :], sem_a.at[0, i])]
+
+        def dy_copy(i):
+            at = rows(i * tm, tm)
+            return [pltpu.make_async_copy(dy_hbm.at[at, :], dy_v.at[at, :], sem_a.at[1, i])]
 
         def w_copies(j):
-            slot = lax.rem(j, 2)
             at = rows(j * c, c, 128)
-            w = [pltpu.make_async_copy(wd_hbm.at[layer, at, :], wd_v.at[slot], sem_w.at[slot, 0])]
+            w = [pltpu.make_async_copy(wd_hbm.at[layer, at, :], wd_v, sem_w.at[0])]
             if not saved:
-                w.append(pltpu.make_async_copy(wg_hbm.at[layer, :, at], wgu_v.at[slot, :, pl.ds(0, c)], sem_w.at[slot, 1]))
-                w.append(pltpu.make_async_copy(wu_hbm.at[layer, :, at], wgu_v.at[slot, :, pl.ds(c, c)], sem_w.at[slot, 2]))
+                w.append(pltpu.make_async_copy(wg_hbm.at[layer, :, at], wgu_v.at[:, pl.ds(0, c)], sem_w.at[1]))
+                w.append(pltpu.make_async_copy(wu_hbm.at[layer, :, at], wgu_v.at[:, pl.ds(c, c)], sem_w.at[2]))
             return w
 
         def s_copies(n):
@@ -588,58 +771,76 @@
                 pltpu.make_async_copy(dgs.at[:, pl.ds(c, c)], dgu_hbm.at[:, rows(f + j * c, c, 128)], sem_o.at[1]),
             ]
 
-        def hid_copy(j):
-            return [pltpu.make_async_copy(hid_hbm.at[:, rows(j * c, c, 128)], hid_v, sem_h)]
+        def hid_copy(k):
+            half = lax.rem(k, 2)
+            return [pltpu.make_async_copy(hid_hbm.at[:, rows(k * c, c, 128)], dgs.at[:, rows(half * c, c, 128)], sem_h.at[half])]
 
         def dw_copy(j):
-            return [pltpu.make_async_copy(dst, dwd_hbm.at[rows(j * c, c), :], sem_o.at[2])]
-
-        start(w_copies(0))
-        for i in range(tiles):
-            start(a_copies(i))
-            if saved and i == 0:
-                start(s_copies(0))
+            n = lax.rem(j, 2) if saved else 0
+            return [pltpu.make_async_copy(dst.at[n], dwd_hbm.at[rows(j * c, c), :], sem_o.at[2 + n])]
+
+        everyone = [partner, across] + [p for _, p in peers]
         if saved:
             start(hid_copy(0))
+            for i in range(tiles):
+                start(dy_copy(i))
+            meet(everyone)
+            start(hid_copy(1))
+            start(w_copies(0))
+            start(s_copies(0))
+            for i in range(tiles):
+                start(a_copy(i))
+            for i in range(tiles):
+                wait(dy_copy(i))
+
+            def down(k, _):
+                half = lax.rem(k, 2)
+                wait(hid_copy(k))
+                for k0, events in at_start.items():
+                    guarded(k == k0, lambda events=events: do(*events))
+
+                @pl.when(k >= 2)
+                def _():
+                    wait(dw_copy(k - 2))
+
+                for p0, w in pieces(c):
+                    dst[half, pl.ds(p0, w), :] = dot(dgs[:, rows(half * c + p0, w, 128)], dy_v[...], TN).astype(BF)
+                start(dw_copy(k))
+
+                @pl.when(k + 2 < CHUNKS)
+                def _():
+                    start(hid_copy(k + 2))
+
+                return 0
+
+            lax.fori_loop(0, CHUNKS, down, 0)
+            wait(dw_copy(CHUNKS - 2))
+            wait(dw_copy(CHUNKS - 1))
+            for i in range(tiles):
+                wait(a_copy(i))
+        else:
+            start(w_copies(0))
+            for i in range(tiles):
+                start(a_copy(i))
+                start(dy_copy(i))
+            meet(everyone)
+
+        def events_at(j, point):
+            for (j0, point0), events in at_chunk.items():
+                if isinstance(point, int):
+                    if point == point0:
+                        guarded(j == j0, lambda events=events: do(*events))
+                elif point0 < 4:
+                    guarded(jnp.logical_and(j == j0, point == point0), lambda events=events: do(*events))
 
         def chunk(j, _):
-            slot = lax.rem(j, 2)
-
-            @pl.when(j >= 3)
-            def _():
-                e4(j - 3)
-
-            @pl.when(j == 2)
-            def _():
-                e2(j - 2, True, False)
-
-            @pl.when(j >= 3)
-            def _():
-                e2(j - 2, False, False)
-
-            @pl.when(j == 1)
-            def _():
-                e0(j - 1, True)
-
-            @pl.when(j >= 2)
-            def _():
-                e0(j - 1, False)
-
             @pl.when(j >= 1)
             def _():
                 wait(o_copies(j - 1))
 
             wait(w_copies(j))
 
-            @pl.when(j + 1 < CHUNKS)
-            def _():
-                start(w_copies(j + 1))
-
             def tile(i, _):
-                @pl.when(j == 0)
-                def _():
-                    wait(a_copies(i))
-
                 if saved:
                     n = j * tiles + i
 
@@ -648,22 +849,21 @@
                         start(s_copies(n + 1))
 
                     wait(s_copies(n))
-
-                @pl.when(jnp.logical_and(i == tiles // 2, j == 1))
-                def _():
-                    e1(j - 1, True, False)
-
-                @pl.when(jnp.logical_and(i == tiles // 2, j >= 2))
-                def _():
-                    e1(j - 1, False, False)
-
+                else:
+
+                    @pl.when(j == 0)
+                    def _():
+                        wait(a_copy(i))
+                        wait(dy_copy(i))
+
+                events_at(j, i)
                 r = rows(i * tm, tm)
                 for p0, w in pieces(c):
                     if not saved:
                         a = a_v[r, :]
-                        both = dot(a, jnp.concatenate([wgu_v[slot, :, pl.ds(p0, w)], wgu_v[slot, :, pl.ds(c + p0, w)]], 1))
+                        both = dot(a, jnp.concatenate([wgu_v[:, pl.ds(p0, w)], wgu_v[:, pl.ds(c + p0, w)]], 1))
                         g, u = both[:, :w], both[:, w:]
-                    dh = dot(dy_v[r, :], wd_v[slot, pl.ds(p0, w), :], NT).astype(BF).astype(F32)
+                    dh = dot(dy_v[r, :], wd_v[pl.ds(p0, w), :], NT).astype(BF).astype(F32)
                     if saved:
                         by_gate, by_up = g_v[lax.rem(n, 2), :, pl.ds(p0, w)], u_v[lax.rem(n, 2), :, pl.ds(p0, w)]
                     else:
@@ -678,56 +878,46 @@
             lax.fori_loop(0, tiles, tile, 0)
             start(o_copies(j))
 
-            @pl.when(j >= 1)
+            @pl.when(j + 1 < CHUNKS)
             def _():
-                wait(dw_copy(j - 1))
-
-            if saved:
-                wait(hid_copy(j))
-            for p0, w in pieces(c):
-                dst[pl.ds(p0, w), :] = dot(hid_v[:, pl.ds(p0, w)], dy_v[...], TN).astype(BF)
-            start(dw_copy(j))
-            if saved:
-
-                @pl.when(j + 1 < CHUNKS)
+                start(w_copies(j + 1))
+
+            events_at(j, 4)
+            if not saved:
+
+                @pl.when(j >= 1)
                 def _():
-                    start(hid_copy(j + 1))
-
-            @pl.when(j >= 2)
-            def _():
-                e3(j - 2, False)
-
+                    wait(dw_copy(j - 1))
+
+                for p0, w in pieces(c):
+                    dst[0, pl.ds(p0, w), :] = dot(hid_v[:, pl.ds(p0, w)], dy_v[...], TN).astype(BF)
+                start(dw_copy(j))
             for k in range(2):
                 stg[pl.ds(k * (d // 2), d // 2), :] = dot(a_v[:, pl.ds(k * (d // 2), d // 2)], dgs[...], TN).astype(BF)
             return 0
 
         lax.fori_loop(0, CHUNKS, chunk, 0)
         wait(o_copies(CHUNKS - 1))
-        wait(dw_copy(CHUNKS - 1))
-
-    bufs = [
-        pltpu.VMEM((t, d), BF),
-        pltpu.VMEM((t, d), BF),
-        pltpu.VMEM((2, c, d), BF),
-        pltpu.VMEM((t, c), BF),
-        pltpu.VMEM((t, 2 * c), BF),
-        pltpu.VMEM((c, d), BF),
-    ]
-    bufs += [pltpu.VMEM((2, tm, c), F32)] * 2 if saved else [pltpu.VMEM((2, d, 2 * c), BF)]
-    bufs += [pltpu.SemaphoreType.DMA((2, tiles)), pltpu.SemaphoreType.DMA((2, 3)), pltpu.SemaphoreType.DMA((3,))]
-    bufs += [pltpu.SemaphoreType.DMA((2, 2)), pltpu.SemaphoreType.DMA] if saved else []
+        if not saved:
+            wait(dw_copy(CHUNKS - 1))
+
+    dma = pltpu.SemaphoreType.DMA
+    bufs = [pltpu.VMEM((t, d), BF), pltpu.VMEM((t, d), BF), pltpu.VMEM((c, d), BF)]
+    bufs += [] if saved else [pltpu.VMEM((t, c), BF)]
+    bufs += [pltpu.VMEM((t, 2 * c), BF), pltpu.VMEM((2 if saved else 1, c, d), BF)]
+    bufs += [pltpu.VMEM((2, tm, c), F32)] * 2 if saved else [pltpu.VMEM((d, 2 * c), BF)]
+    bufs += [dma((2, tiles)), dma((3,)), dma((4,))]
+    bufs += [dma((2, 2)), dma((2,))] if saved else []
     pl.run_scoped(chunks, *bufs)
 
-    ta = t // 8
-
-    def last(wg_v, wu_v, dgu_v, h_v, dy_v, o_v, bg_v, bu_v, own_v, bd_v, ac_v, bx_v, sx_v, br_v, sg_v, sem_w, sem_i, sem_o, dd, dx, dr, dg, dl):
+    ta = t // TILES
+    count = TILES - LEFT if saved else TILES
+
+    def last(wg_v, wu_v, dgu_v, h_v, dy_v, o_v, bg_v, bu_v, sem_w, sem_i, sem_o):
         def i_copy(i, m):
             slot = lax.rem(i, 2)
             part = pl.ds(m * f, f)
-            return pltpu.make_async_copy(dgu_hbm.at[rows(i * ta, ta), part], dgu_v.at[slot, :, part], sem_i.at[slot, m])
-
-        def i_copies(i):
-            return [i_copy(i, 0), i_copy(i, 1)]
+            return [pltpu.make_async_copy(dgu_hbm.at[rows(i * ta, ta), part], dgu_v.at[slot, :, part], sem_i.at[slot, m])]
 
         def h_copies(i):
             slot = lax.rem(i, 2)
@@ -744,157 +934,70 @@
         def w_copy(k):
             return [pltpu.make_async_copy((wg_hbm, wu_hbm)[k].at[layer], (wg_v, wu_v)[k], sem_w.at[k])]
 
-        def dd_copies(k):
-            far = [
-                send(
-                    dwd_hbm.at[rows((2 * m + 1 - core) * own_d + k * rd, rd), :],
-                    bd_v.at[k, m],
-                    (dd.at[0, k, m], dd.at[1, k, m]),
-                    partner,
-                )
-                for m in range(2)
-            ]
-            near = [
-                pltpu.make_async_copy(dwd_hbm.at[rows((2 * m + core) * own_d + k * rd, rd), :], own_v.at[k, m], dl.at[0, k, m])
-                for m in range(2)
-            ]
-            return far + near
-
-        def dx_copies(k):
-            return [send(sx_v.at[k], bx_v.at[k], (dx.at[0, k], dx.at[1, k]), across)]
-
-        def dr_copies(k):
-            return [
-                send(sx_v.at[k, :, rows(n * qd, qd, 128)], br_v.at[k, m], (dr.at[0, k, m], dr.at[1, k, m]), to)
-                for m, (n, to) in enumerate(peers)
-            ]
-
-        def dg_copies(k):
-            at = (rows(k * rd, rd), rows(me_r * qd, qd, 128))
-            far = [send(sg_v.at[k], od_hbm.at[at], (dg.at[0, k, m], dg.at[1, k, m]), to) for m, (_, to) in enumerate(peers)]
-            return far + [pltpu.make_async_copy(sg_v.at[k], od_hbm.at[at], dl.at[1, k, 0])]
-
-        def f0(k):
-            start(dd_copies(k))
-
-        def f1(k):
-            wait(dd_copies(k))
-            ac_v[k] = own_v[k, x].astype(F32) + bd_v[k, x].astype(F32)
-            sx_v[k] = (own_v[k, 1 - x].astype(F32) + bd_v[k, 1 - x].astype(F32)).astype(BF)
-            start(dx_copies(k))
-
-        def f2(k):
-            wait(dx_copies(k))
-            total = ac_v[k] + bx_v[k].astype(F32)
-            ac_v[k] = total
-            sx_v[k] = total.astype(BF)
-            start(dr_copies(k))
-
-        def f3(k):
-            wait(dr_copies(k))
-            total = ac_v[k, :, rows(me_r * qd, qd, 128)]
-            for m in range(3):
-                total = total + br_v[k, m].astype(F32)
-            sg_v[k] = total.astype(BF)
-            start(dg_copies(k))
-
-        def f4(k):
-            wait(dg_copies(k))
-
-        end = CHUNKS - 1
-        todo = {
-            1: [lambda: f1(0), lambda: f1(1)],
-            2: [lambda: e3(end - 1, False), lambda: f1(2)],
-            3: [lambda: f1(3), lambda: f1(4)],
-            5: [lambda: e2(end, False, True), lambda: e4(end - 1)],
-            7: [lambda: f2(0)],
-            8: [lambda: e3(end, True), lambda: f2(1)],
-            10: [lambda: f2(2), lambda: f3(0)],
-            11: [lambda: e4(end), lambda: f3(1)],
-            12: [lambda: f2(3)],
-            13: [lambda: f3(2)],
-            14: [lambda: f2(4)],
-            15: [lambda: f3(3)],
-        }
-
-        def events(i, half):
-            for point, does in todo.items():
-                if point % 2 == half:
-
-                    @pl.when(i == point // 2)
-                    def _(does=does):
-                        for do in does:
-                            do()
-
-        def tail(i):
-            slot = lax.rem(i, 2)
-            by_a = (bg_v[...].astype(F32) + bu_v[...].astype(F32)).astype(BF).astype(F32)
-            wide = h_v[slot].astype(F32)
-            scale = scale_of(wide)
-            by_scale = jnp.sum(by_a * wide, -1, keepdims=True)
-            by_wide = (by_a * scale - (by_scale * scale * scale * scale * (1.0 / d)) * wide).astype(BF)
-            o_v[slot] = (dy_v[slot].astype(F32) + by_wide.astype(F32)).astype(BF)
-
-        def by_g(i):
-            bg_v[...] = dot(dgu_v[lax.rem(i, 2), :, pl.ds(0, f)], wg_v[...], NT).astype(BF)
-
-        def by_u(i):
-            bu_v[...] = dot(dgu_v[lax.rem(i, 2), :, pl.ds(f, f)], wu_v[...], NT).astype(BF)
+        def work(i):
+            n = lax.rem(i, 2)
+            return input_gradient(f, dgu_v.at[n], wg_v, wu_v, h_v.at[1 - n], dy_v.at[1 - n], bg_v, bu_v)
 
         start(w_copy(0))
-        i_copy(0, 0).start()
+        start(i_copy(0, 0))
         start(w_copy(1))
-        i_copy(0, 1).start()
+        start(i_copy(0, 1))
         start(h_copies(0))
-        for p in everyone:
-            pl.semaphore_signal(entered, inc=1, device_id=p, device_id_type=MESH)
-        e4(end - 2)
-        e2(end - 1, False, False)
-        e0(end, False)
-        wait(w_copy(0))
-        i_copy(0, 0).wait()
-        pl.semaphore_wait(entered, 5)
-        for k in range(5):
-            f0(k)
-        e1(end, False, True)
-        start(i_copies(1))
-        by_g(0)
-        events(0, 1)
-        wait(w_copy(1))
-        i_copy(0, 1).wait()
-        by_u(0)
+        do(*at_end[-1])
+
+        def events_at(i, half):
+            for point, events in at_end.items():
+                if point >= 0 and point % 1 == half:
+                    guarded(i == int(point), lambda events=events: do(*events))
 
         def tile(i, _):
-            @pl.when(i + 1 < 8)
+            @pl.when(i + 1 < count)
             def _():
-                start(i_copies(i + 1))
-
-            events(i, 0)
-            wait(i_copies(i))
-            wait(h_copies(i - 1))
+                start(i_copy(i + 1, 0))
+                start(i_copy(i + 1, 1))
+
+            @pl.when(i == 0)
+            def _():
+                wait(w_copy(0))
+
+            wait(i_copy(i, 0))
+
+            @pl.when(i >= 1)
+            def _():
+                start(h_copies(i))
+                wait(h_copies(i - 1))
 
             @pl.when(i >= 3)
             def _():
                 wait(o_copy(i - 3))
 
-            tail(i - 1)
-            by_g(i)
-            start(o_copy(i - 1))
-            start(h_copies(i))
-            events(i, 1)
-            by_u(i)
+            events_at(i, 0)
+            by_gate, by_up, rest = work(i)
+            o_v[lax.rem(i + 1, 2)] = rest()
+            by_gate()
+
+            @pl.when(i >= 1)
+            def _():
+                start(o_copy(i - 1))
+
+            @pl.when(i == 0)
+            def _():
+                wait(w_copy(1))
+
+            wait(i_copy(i, 1))
+            events_at(i, 0.5)
+            by_up()
             return 0
 
-        lax.fori_loop(1, 8, tile, 0)
-        f3(4)
-        wait(h_copies(7))
-        wait(o_copy(5))
-        tail(7)
-        start(o_copy(7))
-        wait(o_copy(6))
-        wait(o_copy(7))
-        for k in range(5):
-            f4(k)
+        lax.fori_loop(0, count, tile, 0)
+        wait(h_copies(count - 1))
+        wait(o_copy(count - 3))
+        _, _, rest = work(count)
+        o_v[(count - 1) % 2] = rest()
+        start(o_copy(count - 1))
+        wait(o_copy(count - 2))
+        wait(o_copy(count - 1))
+        do(*after)
 
     pl.run_scoped(
         last,
@@ -906,21 +1009,9 @@
         pltpu.VMEM((2, ta, d), BF),
         pltpu.VMEM((ta, d), BF),
         pltpu.VMEM((ta, d), BF),
-        pltpu.VMEM((5, 2, rd, d), BF),
-        pltpu.VMEM((5, 2, rd, d), BF),
-        pltpu.VMEM((5, rd, d), F32),
-        pltpu.VMEM((5, rd, d), BF),
-        pltpu.VMEM((5, rd, d), BF),
-        pltpu.VMEM((5, 3, rd, qd), BF),
-        pltpu.VMEM((5, rd, qd), BF),
-        pltpu.SemaphoreType.DMA((2,)),
-        pltpu.SemaphoreType.DMA((2, 4)),
-        pltpu.SemaphoreType.DMA((2,)),
-        pltpu.SemaphoreType.DMA((2, 5, 2)),
-        pltpu.SemaphoreType.DMA((2, 5)),
-        pltpu.SemaphoreType.DMA((2, 5, 3)),
-        pltpu.SemaphoreType.DMA((2, 5, 3)),
-        pltpu.SemaphoreType.DMA((2, 5, 2)),
+        dma((2,)),
+        dma((2, 4)),
+        dma((2,)),
     )
 
 
@@ -928,11 +1019,12 @@
     t, d = a.shape
     f = wd.shape[1]
     c = f // CHUNKS
-    own, dma = d // 4, pltpu.SemaphoreType.DMA
-    shapes = [(t, d), (own, f), (own, f), (f // 4, d), (t, 2 * f), (f, d)]
-    out = pl.pallas_call(
+    own, rd, dma = d // 4, f // 4 // PARTS, pltpu.SemaphoreType.DMA
+    regular = pltpu.SemaphoreType.REGULAR
+    shapes = [(t, d), (own, f), (own, f), (f // 4, d)] + ([(LATE * rd, d)] if saved else []) + [(t, 2 * f), (f, d)]
+    return pl.pallas_call(
         functools.partial(backward_kernel, layer),
-        in_specs=[ANY] * (9 if saved is not None else 6),
+        in_specs=[ANY] * (6 + len(saved)),
         out_specs=[ANY] * len(shapes),
         out_shape=[jax.ShapeDtypeStruct(s, BF) for s in shapes],
         scratch_shapes=[
@@ -949,68 +1041,157 @@
             dma((2, 3)),
             dma((2, 2, 2, 3)),
             dma((2,)),
-            pltpu.SemaphoreType.REGULAR,
-            pltpu.SemaphoreType.REGULAR,
-            pltpu.SemaphoreType.REGULAR((3,)),
-            pltpu.SemaphoreType.REGULAR,
+            regular,
+            regular,
+            regular((3,)),
+            pltpu.VMEM((2, 2, rd, d), BF),
+            pltpu.VMEM((2, 2, rd, d), BF),
+            pltpu.VMEM((2, rd, d), F32),
+            pltpu.VMEM((2, rd, d), BF),
+            pltpu.VMEM((2, rd, d), BF),
+            pltpu.VMEM((2, 3, rd, d // 4), BF),
+            pltpu.VMEM((2, rd, d // 4), BF),
+            dma((2, 2, 2)),
+            dma((2, 2)),
+            dma((2, 2, 3)),
+            dma((2, 2, 3)),
+            dma((2, 2, 2)),
+            regular,
+            regular,
+            regular((3,)),
         ],
         compiler_params=pltpu.CompilerParams(vmem_limit_bytes=VMEM_LIMIT, collective_id=layer, has_side_effects=True),
-        cost_estimate=pl.CostEstimate(
-            flops=(12 if saved is not None else 16) * t * d * f, bytes_accessed=30 * t * f, transcendentals=t * f
-        ),
+        cost_estimate=pl.CostEstimate(flops=(12 if saved else 16) * t * d * f, bytes_accessed=30 * t * f, transcendentals=t * f),
         name=f"backward_{layer}",
-    )(a, h, dy, wg, wu, wd, *(saved or ()))
-    return out[:4]
-
-
-def placed_kernel(*refs):
-    ins, outs = refs[:7], refs[7:11]
-    bufs, sem_in, sem_out = refs[11:18], refs[18], refs[19]
-    parts = 8
-    copies = []
-    for n, (src, buf) in enumerate(zip(ins, bufs, strict=True)):
-        dst = outs[0] if n == 0 else outs[(n + 1) // 2].at[(n - 1) % 2]
-        step = src.shape[0] // (parts if n == 0 else 1)
-        for p in range(parts if n == 0 else 1):
-            at = pl.ds(p * step, step)
-            k = len(copies)
-            copies.append(
-                (
-                    pltpu.make_async_copy(src.at[at, :], buf.at[at, :], sem_in.at[k]),
-                    pltpu.make_async_copy(buf.at[at, :], dst.at[at, :], sem_out.at[k]),
-                )
-            )
-    for first, _ in copies:
-        first.start()
-    for first, second in copies:
-        first.wait()
-        second.start()
-    for _, second in copies:
+    )(a, h, dy, wg, wu, wd, *saved)
+
+
+def last_kernel(n_sums, f, *refs):
+    by_x, dgu, wg, wu, h, dy = refs[:6]
+    sums = refs[6 : 6 + n_sums]
+    outs = refs[6 + n_sums : 10 + n_sums]
+    wg_v, wu_v, dgu_v, h_v, dy_v, o_v, bg_v, bu_v, x_v, *rest = refs[10 + n_sums :]
+    bufs, (sem_w, sem_i, sem_o, sem_in, sem_out) = rest[:n_sums], rest[n_sums:]
+    t, d = by_x.shape
+    ta = t // TILES
+    count = TILES - LEFT
+
+    def i_copy(i, m):
+        at, part = rows((count + i) * ta, ta), pl.ds(m * f, f)
+        return pltpu.make_async_copy(dgu.at[at, part], dgu_v.at[i, :, part], sem_i.at[i, m])
+
+    def h_copies(i):
+        at = rows((count + i) * ta, ta)
+        return [
+            pltpu.make_async_copy(h.at[at, :], h_v.at[i], sem_i.at[i, 2]),
+            pltpu.make_async_copy(dy.at[at, :], dy_v.at[i], sem_i.at[i, 3]),
+        ]
+
+    def o_copy(i):
+        return pltpu.make_async_copy(o_v.at[i], outs[0].at[rows((count + i) * ta, ta), :], sem_o.at[i])
+
+    w_copies = [pltpu.make_async_copy(w.at[0], v, sem_w.at[k]) for k, (w, v) in enumerate(((wg, wg_v), (wu, wu_v)))]
+    w_copies[0].start()
+    i_copy(0, 0).start()
+    w_copies[1].start()
+    i_copy(0, 1).start()
+    moves = [(by_x.at[pl.ds(i * ta, ta), :], x_v.at[pl.ds(i * ta, ta), :], outs[0].at[pl.ds(i * ta, ta), :]) for i in range(count)]
+    at = [(1, 0, 0), (1, 1, 0), (2, 0, 0), (2, 1, 0), (3, 0, 0), (3, 1, 0), (3, 1, outs[3].shape[1] - sums[6].shape[0])]
+    for src, buf, (o, layer, lo) in zip(sums, bufs, at, strict=True):
+        size = outs[o].shape[1] - sums[6].shape[0] if (o, layer, lo) == (3, 1, 0) else src.shape[0]
+        moves.append((src.at[pl.ds(0, size), :], buf.at[pl.ds(0, size), :], outs[o].at[layer, pl.ds(lo, size), :]))
+    moves = [
+        (pltpu.make_async_copy(src, buf, sem_in.at[k]), pltpu.make_async_copy(buf, dst, sem_out.at[k]))
+        for k, (src, buf, dst) in enumerate(moves)
+    ]
+    def take(n):
+        for first, _ in moves[n :: 2 * LEFT]:
+            first.start()
+
+    def give(n):
+        for first, second in moves[n :: 2 * LEFT]:
+            first.wait()
+            second.start()
+
+    def tile(i, _):
+        by_gate, by_up, rest = input_gradient(f, dgu_v.at[i], wg_v, wu_v, h_v.at[i], dy_v.at[i], bg_v, bu_v)
+
+        @pl.when(i == 0)
+        def _():
+            w_copies[0].wait()
+
+        i_copy(i, 0).wait()
+        for n in range(LEFT):
+
+            @pl.when(i == n)
+            def _(n=n):
+                if n > 0:
+                    give(2 * n - 1)
+                take(2 * n)
+
+        by_gate()
+
+        @pl.when(i == 0)
+        def _():
+            w_copies[1].wait()
+
+        i_copy(i, 1).wait()
+        for n in range(LEFT):
+
+            @pl.when(i == n)
+            def _(n=n):
+                give(2 * n)
+                start(h_copies(n))
+                take(2 * n + 1)
+                if n + 1 < LEFT:
+                    i_copy(n + 1, 0).start()
+                    i_copy(n + 1, 1).start()
+
+        by_up()
+        wait(h_copies(i))
+        o_v[i] = rest()
+        o_copy(i).start()
+        return 0
+
+    lax.fori_loop(0, LEFT, tile, 0)
+    give(2 * LEFT - 1)
+    for i in range(LEFT):
+        o_copy(i).wait()
+    for _, second in moves:
         second.wait()
 
 
-def placed(by_x, *sums):
-    ins = (by_x, *sums)
-    outs = [by_x.shape] + [(2, *s.shape) for s in sums[::2]]
+def finish(by_x, dgu, wg, wu, h, dy, *sums):
+    t, d = by_x.shape
+    f = wg.shape[2]
+    ta = t // TILES
+    outs = [(t, d)] + [(2, *sums[n].shape) for n in (0, 2, 4)]
+    tile, dma = pltpu.VMEM((LEFT, ta, d), BF), pltpu.SemaphoreType.DMA
+    moves = TILES - LEFT + len(sums)
     return pl.pallas_call(
-        placed_kernel,
-        in_specs=[ANY] * len(ins),
+        functools.partial(last_kernel, len(sums), f),
+        in_specs=[ANY] * (6 + len(sums)),
         out_specs=[ANY] * len(outs),
         out_shape=[jax.ShapeDtypeStruct(s, BF) for s in outs],
-        scratch_shapes=[pltpu.VMEM(a.shape, BF) for a in ins]
-        + [pltpu.SemaphoreType.DMA((14,)), pltpu.SemaphoreType.DMA((14,))],
+        scratch_shapes=[pltpu.VMEM((d, f), BF), pltpu.VMEM((d, f), BF), pltpu.VMEM((LEFT, ta, 2 * f), BF)]
+        + [tile] * 3
+        + [pltpu.VMEM((ta, d), BF)] * 2
+        + [pltpu.VMEM(((TILES - LEFT) * ta, d), BF)]
+        + [pltpu.VMEM(s.shape, BF) for s in sums]
+        + [dma((2,)), dma((LEFT, 4)), dma((LEFT,)), dma((moves,)), dma((moves,))],
         compiler_params=pltpu.CompilerParams(vmem_limit_bytes=VMEM_LIMIT),
-        name="placed",
-    )(*ins)
+        cost_estimate=pl.CostEstimate(flops=4 * LEFT * ta * d * f, bytes_accessed=16 * t * d, transcendentals=0),
+        name="finish",
+    )(by_x, dgu, wg, wu, h, dy, *sums)
 
 
 def solution(mesh):
     def step(x, dy, *weights):
         x, dy = x[0], dy[0]
         a0, hid, g, u, h, a1, *whole = forward(x, *weights)
-        by_h, *top = backward(a1, h, dy, *whole, None, 1)
-        by_x, *bottom = backward(a0, x, by_h, *whole, (g, u, hid), 0)
-        by_x, *sums = placed(by_x, *(part for pair in zip(bottom, top, strict=True) for part in pair))
+        by_h, g1, u1, d1, _, upper = backward(a1, h, dy, *whole, (), 1)
+        by_x, g0, u0, d0, d1_late, dgu, _ = backward(a0, x, by_h, *whole, (g, u, hid, upper), 0)
+        by_x, *sums = finish(by_x, dgu, *whole[:2], x, by_h, g0, g1, u0, u1, d0, d1, d1_late)
         return (by_x[None], *sums)
 
     states, cut = P(("rep", "r", "s"), None, None), P(None, "s", None)

time: 632 us -> 617 us (0.976)
  Pallas kernels: 624 us -> 609 us
    pallas_call x2, Pallas kernels: 482 us -> 455 us  [backward(): pl.pallas_call(functools.partial(backward_kernel, layer), in_specs=[ANY]...]
    pallas_call x1, Pallas kernels: 13.1 us -> 24.6 us  [finish(): pl.pallas_call(functools.partial(last_kernel, len(sums), f), in_specs=[AN...]
where the time goes in v4:
time: 617 us; the launch traced here: 610 us
  Pallas kernels  609 us (99%)
    pallas_call x2, Pallas kernels, backward(): pl.pallas_call(functools.partial(backward_kernel, layer), in_specs=[ANY]...  455 us
    pallas_call x1, Pallas kernels, forward(): pl.pallas_call(forward_kernel, in_specs=[ANY] * 4, out_specs=[ANY] * len(...  129 us
    pallas_call x1, Pallas kernels, finish(): pl.pallas_call(functools.partial(last_kernel, len(sums), f), in_specs=[AN...  24.6 us

profile of v4, /device:TPU:0, one launch (start us, length us, event | category | flops | bytes accessed | tf_op | source)
XLA Modules:
  0.0 609.9 jit_solution(13533789396350046849)
XLA Ops:
  0.6 129.1 %forward.1 = (bf16[4096,1024]{1,0:T(8,128)(2,1)}, bf16[4096,3200]{1,0:T(8,128)(2,1)}, f32[4096,3200]{1,0:T(8,128)}, f32[4096,3200]{1,0:T(8,128)}, bf16[4096,1024...) custom-call(bf16[4096,1024]{1,0:T(8,128)(2,1)} %bitcast.3, ...), custom_call_target="tpu_custom_call" | custom-call | flops 80530636800 | bytes 209715200 | tf_op jit(solution)/shard_map/forward/pallas_call | solution.py:426
  129.7 257.2 %backward_1.1 = (bf16[4096,1024]{1,0:T(8,128)(2,1)}, bf16[256,3200]{1,0:T(8,128)(2,1)}, bf16[256,3200]{1,0:T(8,128)(2,1)}, bf16[800,1024]{1,0:T(8,128)(2,1)}, bf...) custom-call(bf16[4096,1024]{1,0:T(8,128)(2,1)} %get-tuple-element.29.refs_0_, ...), custom_call_target="tpu_custom_call" | custom-call | flops 214748364800 | bytes 393216000 | tf_op jit(solution)/shard_map/backward_1/pallas_call | solution.py:1025
  386.9 198.2 %backward_0.1 = (bf16[4096,1024]{1,0:T(8,128)(2,1)}, bf16[256,3200]{1,0:T(8,128)(2,1)}, bf16[256,3200]{1,0:T(8,128)(2,1)}, bf16[800,1024]{1,0:T(8,128)(2,1)}, bf...) custom-call(bf16[4096,1024]{1,0:T(8,128)(2,1)} %get-tuple-element.28.refs_0_, ...), custom_call_target="tpu_custom_call" | custom-call | flops 161061273600 | bytes 393216000 | tf_op jit(solution)/shard_map/backward_0/pallas_call | solution.py:1025
  585.1 24.6 %finish.1 = (bf16[4096,1024]{1,0:T(8,128)(2,1)}, bf16[2,256,3200]{2,1,0:T(8,128)(2,1)}, bf16[2,256,3200]{2,1,0:T(8,128)(2,1)}, bf16[2,800,1024]{2,1,0:T(8,128)(2,1)}) custom-call(bf16[4096,1024]{1,0:T(8,128)(2,1)} %get-tuple-element.39.refs_0_, bf16[4096,6400]{1,0:T(8,128)(2,1)} %get-tuple-element.40.refs_1_, ...), custom_call_target="tpu_custom_call" | custom-call | flops 13421772800 | bytes 67108864 | tf_op jit(solution)/shard_map/finish/pallas_call | solution.py:1171
